TPU v7x, 32 devices: a 4x4x1 block of a 4x4x8 slice. The times are simulated.
32 devices in a mesh: dp: 1 (over z), cp: 4 (over y), tp: 8 (over x, core).
Axes of the slice: x: 4, y: 4, z: 1, core: 2. Of those that a mesh axis runs over, the one named last changes fastest.
The devices are a block of a 4x4x8 slice.
Arguments:
- x: bfloat16 [8192, 2048], P(('dp', 'cp', 'tp'))
- g_attn: float32 [2048], replicated
- wq: bfloat16 [2048, 2048], P(None, 'tp')
- wk: bfloat16 [2048, 2048], P(None, 'tp')
- wv: bfloat16 [2048, 2048], P(None, 'tp')
- wo: bfloat16 [2048, 2048], P('tp')
- g_mlp: float32 [2048], replicated
- idx: int32 [8192, 6], P(('dp', 'cp', 'tp'))
- gates: float32 [8192, 6], P(('dp', 'cp', 'tp'))
- w1g: bfloat16 [64, 2048, 1408], P(('cp', 'tp'))
- w1u: bfloat16 [64, 2048, 1408], P(('cp', 'tp'))
- w2: bfloat16 [64, 1408, 2048], P(('cp', 'tp'))
- ws1g: bfloat16 [2048, 2816], P(None, 'tp')
- ws1u: bfloat16 [2048, 2816], P(None, 'tp')
- ws2: bfloat16 [2816, 2048], P('tp')
Outputs:
- output: bfloat16 [8192, 2048], P(('dp', 'cp', 'tp'))
All inputs are finite; a program needn't handle non-finite values.
Results may differ from a plain program's by a relative error of at most 0.0132251.
Values are sent between devices in bfloat16 or wider.
A program may use at most 768 MiB of HBM per device.

v0:
```python
import jax
import jax.numpy as jnp
from jax import lax
from jax.sharding import PartitionSpec as P

HEAD = 128
EPS = 1e-6
ROPE_BASE = 10000.0


def rms_norm(a, g):
    af = a.astype(jnp.float32)
    r = af * lax.rsqrt(jnp.mean(af * af, axis=-1, keepdims=True) + EPS)
    return (r * g).astype(jnp.bfloat16)


def rope(t, pos):
    half = t.shape[-1] // 2
    freq = ROPE_BASE ** (-jnp.arange(half, dtype=jnp.float32) / half)
    ang = pos.astype(jnp.float32)[:, None] * freq[None, :]
    c = jnp.cos(ang)[:, None, :]
    s = jnp.sin(ang)[:, None, :]
    t1 = t[..., :half]
    t2 = t[..., half:]
    return jnp.concatenate([t1 * c - t2 * s, t2 * c + t1 * s], axis=-1)


def layout_pos(i, ncp, seq):
    half = seq // (2 * ncp)
    r = i // (2 * half)
    w = i % (2 * half)
    return jnp.where(w < half, r * half + w, (2 * ncp - 1 - r) * half + w - half)


def solution(mesh):
    ncp = mesh.shape["cp"]
    ntp = mesh.shape["tp"]
    ndev = ncp * ntp
    f32 = jnp.float32
    bf16 = jnp.bfloat16
    rows = P(("dp", "cp", "tp"), None)
    cols = P(None, "tp")
    wrows = P("tp", None)
    rep = P(None)
    exps = P(("cp", "tp"), None, None)

    def layer(x, g_attn, wq, wk, wv, wo, g_mlp, idx, gates, w1g, w1u, w2, ws1g, ws1u, ws2):
        r = lax.axis_index("cp")
        ntok, dm = x.shape
        seq = ntok * ndev
        nloc = seq // ncp
        nle = w1g.shape[0]
        num_e = nle * ndev
        top = idx.shape[1]
        cap = top * (2 * ntok // num_e + 1)
        nq = wq.shape[1] // HEAD
        nkvv = wk.shape[1] // HEAD
        grp = nq // nkvv

        xg = lax.all_gather(rms_norm(x, g_attn), "tp", axis=0, tiled=True)
        pos_q = layout_pos(r * nloc + jnp.arange(nloc), ncp, seq)
        pos_k = layout_pos(jnp.arange(seq), ncp, seq)
        q = rope(jnp.dot(xg, wq, preferred_element_type=f32).reshape(nloc, nq, HEAD), pos_q)
        q = q.astype(bf16).reshape(nloc, nkvv, grp, HEAD)
        k = rope(jnp.dot(xg, wk, preferred_element_type=f32).reshape(nloc, nkvv, HEAD), pos_q).astype(bf16)
        v = jnp.dot(xg, wv, preferred_element_type=f32).astype(bf16).reshape(nloc, nkvv, HEAD)
        k_all = lax.all_gather(k, "cp", axis=0, tiled=True)
        v_all = lax.all_gather(v, "cp", axis=0, tiled=True)
        s = jnp.einsum("qngd,knd->ngqk", q, k_all, preferred_element_type=f32) * HEAD ** -0.5
        mask = pos_k[None, :] <= pos_q[:, None]
        pr = jax.nn.softmax(jnp.where(mask[None, None], s, -1e30), axis=-1)
        o = jnp.einsum("ngqk,knd->qngd", pr.astype(bf16), v_all, preferred_element_type=f32)
        o = o.astype(bf16).reshape(nloc, nq * HEAD)
        attn = lax.psum_scatter(jnp.dot(o, wo, preferred_element_type=f32), "tp", scatter_dimension=0, tiled=True)
        h = (x.astype(f32) + attn).astype(bf16)
        t = rms_norm(h, g_mlp)

        tg = lax.all_gather(t, "tp", axis=0, tiled=True)
        u = (jax.nn.silu(jnp.dot(tg, ws1g, preferred_element_type=f32)) * jnp.dot(tg, ws1u, preferred_element_type=f32)).astype(bf16)
        shared = lax.psum_scatter(jnp.dot(u, ws2, preferred_element_type=f32), "tp", scatter_dimension=0, tiled=True)

        e_flat = idx.reshape(-1)
        onehot = (e_flat[:, None] == jnp.arange(num_e)[None, :]).astype(jnp.int32)
        rank = jnp.sum((jnp.cumsum(onehot, axis=0) - onehot) * onehot, axis=1)
        slot = e_flat * cap + rank
        src = jnp.full((num_e * cap,), ntok, jnp.int32).at[slot].set(jnp.arange(ntok * top) // top)
        tpad = jnp.concatenate([t, jnp.zeros((1, dm), bf16)], axis=0)
        send = tpad[src].reshape(ncp, ntp, nle * cap, dm)
        recv = lax.all_to_all(send, "tp", 1, 1, tiled=True)
        recv = lax.all_to_all(recv, "cp", 0, 0, tiled=True)
        xin = recv.reshape(ndev, nle, cap, dm).transpose(1, 0, 2, 3).reshape(nle, ndev * cap, dm)
        a = jnp.einsum("lnh,lhf->lnf", xin, w1g, preferred_element_type=f32)
        b = jnp.einsum("lnh,lhf->lnf", xin, w1u, preferred_element_type=f32)
        z = jnp.einsum("lnf,lfh->lnh", (jax.nn.silu(a) * b).astype(bf16), w2, preferred_element_type=f32).astype(bf16)
        back = z.reshape(nle, ndev, cap, dm).transpose(1, 0, 2, 3).reshape(ncp, ntp, nle * cap, dm)
        back = lax.all_to_all(back, "cp", 0, 0, tiled=True)
        back = lax.all_to_all(back, "tp", 1, 1, tiled=True)
        zc = back.reshape(num_e * cap, dm)[slot].reshape(ntok, top, dm)
        routed = jnp.sum(gates[:, :, None] * zc.astype(f32), axis=1)
        return (h.astype(f32) + shared + routed).astype(bf16)

    return jax.shard_map(layer, mesh=mesh,
                         in_specs=(rows, rep, cols, cols, cols, wrows, rep, rows, rows, exps, exps, exps, cols, cols, wrows),
                         out_specs=rows, check_vma=False)
```

profile of v0, /device:TPU:97, one launch (start us, length us, event | category | flops | bytes accessed | tf_op | source)
XLA Modules:
  0.0 1420.5 jit_solution(4010414087767195266)
XLA Ops:
  16.4 45.7 %all-gather.5.cloned.1.call-done = bf16[2048,2048]{1,0:T(8,128)(2,1)} async-done(((bf16[256,2048]{1,0:T(8,128)(2,1)}), bf16[2048,2048]{1,0:T(8,128)(2,1)}) %all-gather.5.cloned.1.call-update) | async-done | bytes 8388624 | tf_op jit(solution)/shard_map/all_gather | solution.py:60
  126.8 14.5 %all-gather.9.cloned.1.call-done = bf16[8192,2,128]{2,0,1:T(8,128)(2,1)} async-done(((bf16[2048,2,128]{2,0,1:T(8,128)(2,1)}), bf16[8192,2,128]{2,0,1:T(8,128)(2,1)}) %all-gather.9.cloned.1.call-update) | async-done | bytes 4194320 | tf_op jit(solution)/shard_map/all_gather | solution.py:67
  141.4 52.4 %fusion.1 = (f32[2,2048]{1,0:T(2,128)S(1)}, f32[2,8192,2048]{2,1,0:T(8,128)}) fusion(pred[2048,8192]{0,1:T(8,128)(4,1)} %broadcast_compare_fusion, bf16[8192,2,128]{2,0,1:T(8,128)(2,1)} %all-gather.9.cloned.1.call-done, bf16[2048,2,64]{2,0,1:T(8,128)(2,1)S(1)} %copy-done.5, bf16[2048,2,64]{2,0,1:T(8,128)(2,1)S(1)} %copy-done.4), kind=kOutput, calls=%fused_computation.7 | convolution fusion | flops 8692690944 | bytes 156254208 | tf_op jit(solution)/shard_map/qngd,knd->ngqk/dot_general | solution.py:69
  193.8 46.8 %fusion = f32[2,2048]{1,0:T(2,128)} fusion(f32[2,8192,2048]{2,1,0:T(8,128)} %get-tuple-element.20, f32[2,2048]{1,0:T(2,128)S(1)} %get-tuple-element.19, pred[2048,8192]{0,1:T(8,128)(4,1)} %broadcast_compare_fusion), kind=kLoop, calls=%fused_computation.6 | loop fusion | flops 134213632 | bytes 151027712 | tf_op jit(solution)/shard_map/reduce_sum | solution.py:71
  240.6 54.8 %fusion.5 = bf16[2,128,2048]{2,1,0:T(8,128)(2,1)S(1)} fusion(bf16[8192,2,128]{0,2,1:T(8,128)(2,1)} %all-gather.7.cloned.1.call-done, f32[2,2048]{1,0:T(2,128)} %fusion, f32[2,2048]{1,0:T(2,128)S(1)} %get-tuple-element.19, f32[2,8192,2048]{2,1,0:T(8,128)} %get-tuple-element.20, pred[2048,8192]{0,1:T(8,128)(4,1)} %broadcast_compare_fusion), kind=kOutput, calls=%fused_computation.23 | convolution fusion | flops 8758231040 | bytes 156270592 | tf_op jit(solution)/shard_map/ngqk,knd->qngd/dot_general | solution.py:72
  305.6 18.5 %reduce-window.6 = s32[64,12,128]{2,1,0:T(8,128)S(1)} reduce-window(s32[64,12,128]{2,1,0:T(8,128)S(1)} %fusion.22, s32[]{:T(128)} %constant.91.clone.1), window={size=1x1x128 pad=0_0x0_0x127_0}, to_apply=%region_6.7 | reduce-window | flops 12484608 | bytes 786436 | tf_op jit(solution)/shard_map/reduce-window
  332.7 60.6 %reduce-scatter.3.cloned.1.call-done = f32[256,2048]{1,0:T(8,128)} async-done(((f32[2048,2048]{1,0:T(8,128)}), f32[256,2048]{1,0:T(8,128)}) %reduce-scatter.3.cloned.1.call-update) | async-done | bytes 2097168 | tf_op jit(solution)/shard_map/reduce_scatter | solution.py:74
  413.9 16.8 %reshape.281 = bf16[4,8,108,2048]{3,2,1,0:T(8,128)(2,1)} reshape(bf16[3456,2048]{1,0:T(8,128)(2,1)} %gather_fusion) | data formatting | bytes 28311552 | tf_op jit(solution)/shard_map/reshape | solution.py:88
  430.6 17.9 %copy.48 = bf16[4,8,108,2048]{3,0,2,1:T(4,128)(2,1)} copy(bf16[4,8,108,2048]{3,2,1,0:T(8,128)(2,1)} %reshape.281) | data formatting | bytes 28311552 | tf_op jit(solution)/shard_map/reshape | solution.py:88
  455.6 188.5 %all-to-all-done = bf16[4,8,108,2048]{3,0,2,1:T(4,128)(2,1)} async-done(((bf16[4,8,108,2048]{3,0,2,1:T(4,128)(2,1)}), bf16[4,8,108,2048]{3,0,2,1:T(4,128)(2,1)}, u32[]{:S(2)}, u32[]{:S(2)}) %all-to-all-start) | async-done | bytes 14155808 | tf_op jit(solution)/shard_map/all_to_all | solution.py:89
  644.1 16.3 %copy.49 = bf16[4,8,108,2048]{3,1,2,0:T(8,128)(2,1)} copy(bf16[4,8,108,2048]{3,0,2,1:T(4,128)(2,1)} %all-to-all-done) | data formatting | bytes 28311552 | tf_op jit(solution)/shard_map/all_to_all | solution.py:89
  675.4 14.5 %fusion.17 = f32[2048,2048]{1,0:T(8,128)} fusion(bf16[352,2048]{1,0:T(8,128)(2,1)S(1)} %copy-done, bf16[2048,2048]{1,0:T(8,128)(2,1)} %all-gather.11.cloned.1.call-done, bf16[2048,352]{0,1:T(8,128)(2,1)} %param.28, f32[2048,352]{0,1:T(8,128)} %fusion.63), kind=kOutput, calls=%fused_computation.39 | convolution fusion | flops 5909905408 | bytes 30932992 | tf_op jit(solution)/shard_map/dot_general | solution.py:80
  690.0 131.5 %all-to-all-done.1 = bf16[4,8,108,2048]{3,1,2,0:T(8,128)(2,1)} async-done(((bf16[4,8,108,2048]{3,1,2,0:T(8,128)(2,1)}), bf16[4,8,108,2048]{3,1,2,0:T(8,128)(2,1)}, u32[]{:S(2)}, u32[]{:S(2)}) %all-to-all-start.1) | async-done | bytes 14155808 | tf_op jit(solution)/shard_map/all_to_all | solution.py:90
  839.0 17.3 %reshape.283 = bf16[2,1728,2048]{2,1,0:T(8,128)(2,1)} reshape(bf16[2,32,54,2048]{3,2,1,0:T(8,128)(2,1)} %copy.51) | data formatting | bytes 28311552 | tf_op jit(solution)/shard_map/reshape | solution.py:91
  856.3 30.8 %fusion.64 = f32[2,1728,1408]{2,1,0:T(8,128)} fusion(bf16[2,1728,2048]{2,1,0:T(8,128)(2,1)} %reshape.283, bf16[2,2048,1408]{2,1,0:T(8,128)(2,1)} %param.24), kind=kOutput, calls=%fused_computation.114 | convolution fusion | flops 19931332608 | bytes 45154304 | tf_op jit(solution)/shard_map/lnh,lhf->lnf/dot_general | solution.py:92
  887.1 32.6 %multiply_convert_fusion = bf16[2,1728,1408]{2,1,0:T(8,128)(2,1)} fusion(f32[2,1728,1408]{2,1,0:T(8,128)} %fusion.64, bf16[2,1728,2048]{2,1,0:T(8,128)(2,1)} %reshape.283, bf16[2,2048,1408]{2,1,0:T(8,128)(2,1)} %param.25), kind=kOutput, calls=%fused_computation.11 | convolution fusion | flops 19960528896 | bytes 54886400 | tf_op jit(solution)/shard_map/lnh,lhf->lnf/dot_general | solution.py:93
  919.8 29.2 %convolution_convert_fusion = bf16[2,1728,2048]{2,1,0:T(8,128)(2,1)} fusion(bf16[2,1728,1408]{2,1,0:T(8,128)(2,1)} %multiply_convert_fusion, bf16[2,1408,2048]{2,1,0:T(8,128)(2,1)} %param.26), kind=kOutput, calls=%fused_computation.13 | convolution fusion | flops 19938410496 | bytes 35422208 | tf_op jit(solution)/shard_map/lnf,lfh->lnh/dot_general | solution.py:94
  948.9 17.2 %reshape.284 = bf16[2,32,54,2048]{3,2,1,0:T(8,128)(2,1)} reshape(bf16[2,1728,2048]{2,1,0:T(8,128)(2,1)} %convolution_convert_fusion) | data formatting | bytes 28311552 | tf_op jit(solution)/shard_map/reshape | solution.py:95
  981.6 156.5 %all_to_all.20 = bf16[4,8,108,2048]{3,1,2,0:T(8,128)(2,1)S(1)} all-to-all(bf16[4,8,108,2048]{3,1,2,0:T(8,128)(2,1)S(1)} %copy.53), channel_id=1, replica_groups=mesh['dp'=1,'cp'=4,'tp'=8] {'cp'}, dimensions={0} | all-to-all | bytes 28311552 | tf_op jit(solution)/shard_map/all_to_all | solution.py:96
  1138.1 32.3 %copy.54 = bf16[4,8,108,2048]{3,0,2,1:T(4,128)(2,1)} copy(bf16[4,8,108,2048]{3,1,2,0:T(8,128)(2,1)S(1)} %all_to_all.20) | data formatting | bytes 28311552 | tf_op jit(solution)/shard_map/all_to_all | solution.py:96
  1179.3 155.2 %all-to-all-done.3 = bf16[4,8,108,2048]{3,0,2,1:T(4,128)(2,1)} async-done(((bf16[4,8,108,2048]{3,0,2,1:T(4,128)(2,1)}), bf16[4,8,108,2048]{3,0,2,1:T(4,128)(2,1)}, u32[]{:S(2)}, u32[]{:S(2)}) %all-to-all-start.3) | async-done | bytes 14155808 | tf_op jit(solution)/shard_map/all_to_all | solution.py:97
  1334.6 16.5 %copy.55 = bf16[4,8,108,2048]{3,2,1,0:T(8,128)(2,1)} copy(bf16[4,8,108,2048]{3,0,2,1:T(4,128)(2,1)} %all-to-all-done.3) | data formatting | bytes 28311552 | tf_op jit(solution)/shard_map/all_to_all | solution.py:97
  1351.1 16.9 %reshape.286 = bf16[3456,2048]{1,0:T(8,128)(2,1)} reshape(bf16[4,8,108,2048]{3,2,1,0:T(8,128)(2,1)} %copy.55) | data formatting | bytes 28311552 | tf_op jit(solution)/shard_map/reshape | solution.py:98
  1367.9 19.5 %gather_fusion.1 = bf16[1536,2048]{1,0:T(8,128)(2,1)} fusion(bf16[3456,2048]{1,0:T(8,128)(2,1)} %reshape.286, s32[2048]{0:T(1024)S(1)} %pad_clamp_fusion.1), kind=kCustom, calls=%fused_computation.1 | custom fusion | bytes 12589056 | tf_op jit(solution)/shard_map/gather | solution.py:98
  (98 shorter events, 203.4 us)
Async XLA Ops:
  6.5 668.9 %copy-start = (bf16[352,2048]{1,0:T(8,128)(2,1)S(1)}, bf16[352,2048]{1,0:T(8,128)(2,1)}, u32[]{:S(2)}) copy-start(bf16[352,2048]{1,0:T(8,128)(2,1)} %param.29) | copy-start | bytes 4325380
  6.6 55.6 %all-gather.5.cloned.1.call-start = ((), (), s32[]{:S(2)}) async-start(), calls=%async_computation.6 | async-start | bytes 9437184 | tf_op jit(solution)/shard_map/all_gather | solution.py:60
  10.8 130.6 %all-gather.9.cloned.1.call-start = ((), (), s32[]{:S(2)}) async-start(), calls=%async_computation.8 | async-start | bytes 5242880 | tf_op jit(solution)/shard_map/all_gather | solution.py:67
  96.1 144.5 %all-gather.7.cloned.1.call-start = ((), (), s32[]{:S(2)}) async-start(), calls=%async_computation.7 | async-start | bytes 5242880 | tf_op jit(solution)/shard_map/all_gather | solution.py:68
  107.0 12.8 copy-start.12
  119.8 21.6 %copy-start.4 = (bf16[2048,2,64]{2,0,1:T(8,128)(2,1)S(1)}, bf16[2048,2,64]{2,0,1:T(8,128)(2,1)}, u32[]{:S(2)}) copy-start(bf16[2048,2,64]{2,0,1:T(8,128)(2,1)} %get-tuple-element.7) | copy-start | bytes 1572868
  119.8 21.6 %copy-start.5 = (bf16[2048,2,64]{2,0,1:T(8,128)(2,1)S(1)}, bf16[2048,2,64]{2,0,1:T(8,128)(2,1)}, u32[]{:S(2)}) copy-start(bf16[2048,2,64]{2,0,1:T(8,128)(2,1)} %get-tuple-element.8) | copy-start | bytes 1572868
  126.7 266.6 %reduce-scatter.3.cloned.1.call-start = ((), (), s32[]{:S(2)}) async-start(), calls=%async_computation.9 | async-start | bytes 18874368 | tf_op jit(solution)/shard_map/reduce_scatter | solution.py:74
  240.6 54.8 %copy-start.6 = (bf16[256,2048]{1,0:T(8,128)(2,1)S(1)}, bf16[256,2048]{1,0:T(8,128)(2,1)}, u32[]{:S(2)}) copy-start(bf16[256,2048]{1,0:T(8,128)(2,1)} %param.20) | copy-start | bytes 3145732
  303.6 0.7 copy-start.7
  303.6 89.7 %copy-start.1 = (bf16[256,2048]{1,0:T(8,128)(2,1)S(1)}, bf16[256,2048]{1,0:T(8,128)(2,1)}, u32[]{:S(2)}) copy-start(bf16[256,2048]{1,0:T(8,128)(2,1)} %param.15) | copy-start | bytes 3145732
  325.9 0.6 copy-start.8
  395.3 1.0 copy-start.2
  448.5 195.6 %all-to-all-start = ((bf16[4,8,108,2048]{3,0,2,1:T(4,128)(2,1)}), bf16[4,8,108,2048]{3,0,2,1:T(4,128)(2,1)}, u32[]{:S(2)}, u32[]{:S(2)}) async-start(bf16[4,8,108,2048]{3,0,2,1:T(4,128)(2,1)} %copy.48), calls=%async_computation.2 | async-start | bytes 28311552 | tf_op jit(solution)/shard_map/all_to_all | solution.py:89
  455.0 212.3 %all-gather.11.cloned.1.call-start = ((), (), s32[]{:S(2)}) async-start(), calls=%async_computation.10 | async-start | bytes 9437184 | tf_op jit(solution)/shard_map/all_gather | solution.py:78
  660.4 6.9 copy-start.11
  660.4 161.1 %all-to-all-start.1 = ((bf16[4,8,108,2048]{3,1,2,0:T(8,128)(2,1)}), bf16[4,8,108,2048]{3,1,2,0:T(8,128)(2,1)}, u32[]{:S(2)}, u32[]{:S(2)}) async-start(bf16[4,8,108,2048]{3,1,2,0:T(8,128)(2,1)} %copy.49), calls=%async_computation.3 | async-start | bytes 28311552 | tf_op jit(solution)/shard_map/all_to_all | solution.py:90
  667.2 742.6 %reduce-scatter.5.cloned.1.call-start = ((), (), s32[]{:S(2)}) async-start(), calls=%async_computation.11 | async-start | bytes 18874368 | tf_op jit(solution)/shard_map/reduce_scatter | solution.py:80
  1170.4 8.7 copy-start.10
  1170.4 8.9 copy-start.9
  1170.4 164.1 %all-to-all-start.3 = ((bf16[4,8,108,2048]{3,0,2,1:T(4,128)(2,1)}), bf16[4,8,108,2048]{3,0,2,1:T(4,128)(2,1)}, u32[]{:S(2)}, u32[]{:S(2)}) async-start(bf16[4,8,108,2048]{3,0,2,1:T(4,128)(2,1)} %copy.54), calls=%async_computation.5 | async-start | bytes 28311552 | tf_op jit(solution)/shard_map/all_to_all | solution.py:97
  1399.1 10.6 copy-start.3
Sparse Core Ops, SparseCore 0:
  10.9 51.2 all-gather.4
  96.2 45.1 all-gather.8
  142.9 45.9 all-gather.6
  303.8 89.4 reduce-scatter.2
  457.1 95.5 all-gather.10
  690.1 88.8 reduce-scatter.4
where the time goes:
time: 1430 us; the launch traced here: 1420 us
  waiting for transfers between devices  597 us (42%)
  local copies, waits for them, and re-layouts  256 us (18%)
  matrix products  249 us (17%)
  blocking collectives  157 us (11%)
  other arithmetic  115 us (8%)
  starting transfers between devices  33 us (2%)
    all_to_all x1, waiting for transfers between devices, layer(): recv = lax.all_to_all(send, 'tp', 1, 1, tiled=True)  188 us
    all_to_all x1, blocking collectives, layer(): back = lax.all_to_all(back, 'cp', 0, 0, tiled=True)  157 us
    all_to_all x1, waiting for transfers between devices, layer(): back = lax.all_to_all(back, 'tp', 1, 1, tiled=True)  155 us
    all_to_all x1, waiting for transfers between devices, layer(): recv = lax.all_to_all(recv, 'cp', 0, 0, tiled=True)  132 us
    reduce_scatter x1, waiting for transfers between devices, layer(): lax.psum_scatter(jnp.dot(o, wo, preferred_element_type=f32), 'tp', scatte...  60.6 us
    dot_general x1, matrix products, layer(): jnp.einsum('ngqk,knd->qngd', pr.astype(bf16), v_all, preferred_element_ty...  54.8 us
    dot_general x1, matrix products, layer(): jnp.einsum('qngd,knd->ngqk', q, k_all, preferred_element_type=f32)  52.4 us
    reduce_sum x1, other arithmetic, layer(): pr = jax.nn.softmax(jnp.where(mask[None, None], s, -1e+30), axis=-1)  46.8 us
  transfers between devices with their start and end apart: 9, of which 6 were waited for; matrix products, arithmetic and copies ran while one was open for 32% of the time, Pallas kernels for 0%

commit v1 on v0

v1 whole, which is shorter than its diff:
```python
import functools

import jax
import jax.numpy as jnp
from jax import lax
from jax.experimental import pallas as pl
from jax.experimental.pallas import tpu as pltpu
from jax.sharding import PartitionSpec as P

HEAD = 128
EPS = 1e-6
ROPE_BASE = 10000.0
MESH = pl.DeviceIdType.MESH
VMEM_MAX = 66_500_000
f32 = jnp.float32
bf16 = jnp.bfloat16


def rms_norm(a, g):
    af = a.astype(f32)
    r = af * lax.rsqrt(jnp.mean(af * af, axis=-1, keepdims=True) + EPS)
    return (r * g).astype(bf16)


def layout_pos(i, ncp, seq):
    half = seq // (2 * ncp)
    r = i // (2 * half)
    w = i % (2 * half)
    return jnp.where(w < half, r * half + w, (2 * ncp - 1 - r) * half + w - half)


def qkv_kernel(x_ref, wq_ref, wk_ref, wv_ref, c_ref, s_ref, q_ref, kv_ref):
    xb = x_ref[...]
    c, s = c_ref[...], s_ref[...]
    width = wq_ref.shape[1]

    def put(w_ref, o_ref, at, turn):
        r = jnp.dot(xb, w_ref[...], preferred_element_type=f32)
        for hd in range(width // HEAD):
            a = r[:, hd * HEAD:(hd + 1) * HEAD]
            if turn:
                a = a * c + pltpu.roll(a, HEAD // 2, 1) * s
            o_ref[:, at + hd * HEAD:at + (hd + 1) * HEAD] = a.astype(bf16)

    put(wk_ref, kv_ref, 0, True)
    put(wv_ref, kv_ref, width, False)
    put(wq_ref, q_ref, 0, True)


def qkv(xg, wq, wk, wv, cos, sin):
    n, dm = xg.shape
    w = wq.shape[1]
    blk = 512
    whole = lambda a, b: pl.BlockSpec((a, b), lambda i: (0, 0))
    rowb = lambda b: pl.BlockSpec((blk, b), lambda i: (i, 0))
    return pl.pallas_call(
        qkv_kernel,
        grid=(n // blk,),
        in_specs=[rowb(dm), whole(dm, w), whole(dm, w), whole(dm, w), rowb(HEAD), rowb(HEAD)],
        out_specs=[rowb(w), rowb(2 * w)],
        out_shape=[jax.ShapeDtypeStruct((n, w), bf16), jax.ShapeDtypeStruct((n, 2 * w), bf16)],
        compiler_params=pltpu.CompilerParams(vmem_limit_bytes=48 * 2**20),
        cost_estimate=pl.CostEstimate(flops=6 * n * dm * w, bytes_accessed=2 * n * dm + 6 * dm * w + 6 * n * w, transcendentals=0),
    )(xg, wq, wk, wv, cos, sin)


def attn_kernel(ncp, piece, bq, bk, q_ref, k_ref, v_ref, o_ref, m_ref, l_ref, acc_ref):
    r = lax.axis_index("cp")
    qi = pl.program_id(1)
    per = piece // bq
    second = qi // per
    pq = jnp.where(second == 0, r, 2 * ncp - 1 - r)
    inner = qi % per
    scale = HEAD ** -0.5
    q = q_ref[...]
    m_ref[...] = jnp.full_like(m_ref, -1e30)
    l_ref[...] = jnp.zeros_like(l_ref)
    acc_ref[...] = jnp.zeros_like(acc_ref)

    def step(row, mask_off):
        row = pl.multiple_of(row, bk)
        k = k_ref[pl.ds(row, bk), :]
        v = v_ref[pl.ds(row, bk), :]
        s = lax.dot_general(q, k, (((1,), (1,)), ((), ())), preferred_element_type=f32)
        if mask_off is not None:
            qp = lax.broadcasted_iota(jnp.int32, s.shape, 0) + mask_off
            kp = lax.broadcasted_iota(jnp.int32, s.shape, 1)
            s = jnp.where(kp <= qp, s, -1e30)
        m_old = m_ref[:, :1]
        m_new = jnp.maximum(m_old, jnp.max(s, axis=1, keepdims=True))
        p = jnp.exp((s - m_new) * scale)
        a = jnp.exp((m_old - m_new) * scale)
        l_ref[...] = a * l_ref[...] + jnp.sum(p, axis=1, keepdims=True)
        acc_ref[...] = a * acc_ref[...] + jnp.dot(p.astype(bf16), v, preferred_element_type=f32)
        m_ref[...] = jnp.broadcast_to(m_new, m_ref.shape)

    def base_of(p):
        return jnp.where(p < ncp, p * (2 * piece), (2 * ncp - 1 - p) * (2 * piece) + piece)

    kper = piece // bk

    def full_piece(p, _):
        b = base_of(p)
        for j in range(kper):
            step(b + j * bk, None)
        return 0

    lax.fori_loop(0, pq, full_piece, 0)
    b = base_of(pq)
    first = inner * bq
    lax.fori_loop(0, first // bk, lambda j, _: (step(b + j * bk, None), 0)[1], 0)
    for j in range(max(bq // bk, 1)):
        at = first // bk * bk + j * bk
        step(b + at, first - at)
    o_ref[...] = (acc_ref[...] / l_ref[...]).astype(bf16)


def attention(q, kv, ncp):
    n, w = q.shape
    seq = kv.shape[0]
    heads = w // HEAD
    piece = n // 2
    bq, bk = 512, 512
    return pl.pallas_call(
        functools.partial(attn_kernel, ncp, piece, bq, bk),
        grid=(heads, n // bq),
        in_specs=[pl.BlockSpec((bq, HEAD), lambda h, i: (i, h)),
                  pl.BlockSpec((seq, HEAD), lambda h, i: (0, h)),
                  pl.BlockSpec((seq, HEAD), lambda h, i: (0, heads + h))],
        out_specs=pl.BlockSpec((bq, HEAD), lambda h, i: (i, h)),
        out_shape=jax.ShapeDtypeStruct((n, w), bf16),
        scratch_shapes=[pltpu.VMEM((bq, HEAD), f32)] * 3,
        compiler_params=pltpu.CompilerParams(vmem_limit_bytes=40 * 2**20),
        cost_estimate=pl.CostEstimate(flops=4 * n * seq * w, bytes_accessed=6 * seq * w, transcendentals=n * seq),
    )(q, kv, kv)


ORDER = [(0, 0), (1, 0), (3, 0), (0, 1), (0, 3), (2, 0), (0, 2), (1, 1),
         (1, 3), (3, 1), (3, 3), (2, 1), (2, 3), (1, 2), (3, 2), (2, 2)]
DIST = [0, 1, 2, 1]


def packed(values):
    return [sum(v << (2 * i) for i, v in enumerate(values[k:k + 8])) for k in (0, 8)]


DX, DY = packed([o[0] for o in ORDER]), packed([o[1] for o in ORDER])


def look(table, j):
    a, b = table
    return ((a + (j // 8) * (b - a)) >> (2 * (j % 8))) & 3


def gather_copies(rows):
    h, q = rows // 2, rows // 4
    out = []
    for flip in (False, True):
        base = h if flip else 0
        fw = (lambda a, b: (b, a)) if flip else (lambda a, b: (a, b))

        def add(blk, lo, n, step):
            out.append((fw(*blk), base + lo, n, fw(*step)))

        add((0, 0), 0, h, (1, 0))
        add((0, 0), 0, h, (3, 0))
        add((3, 0), 0, q, (1, 0))
        add((1, 0), q, q, (3, 0))
        for b in range(4):
            add((b, 0), 0, h, (0, 1))
            add((b, 0), 0, h, (0, 3))
            add((b, 3), 0, q, (0, 1))
            add((b, 1), q, q, (0, 3))
    return out


def dist(b):
    return DIST[b[0]] + DIST[b[1]]


def moe_kernel(nx, ny, cap, groups, t_ref, mc_ref, code_ref, gate_ref, w1g_ref, w1u_ref, w2_ref,
               acc_ref, tg_ref, rz_ref,
               vg, vu, vd, xin, act, zb, tb, zin,
               wsem, tsem, zsem, lsem, ag_s, ag_r, dd_s, dd_r, rt_s, rt_r):
    ntok, dm = t_ref.shape
    ff = w1g_ref.shape[2]
    y = lax.axis_index("cp")
    tp = lax.axis_index("tp")
    x, c = tp // 2, tp % 2
    nchip = nx * ny
    per = nchip // groups
    homes = 2 * per

    def dev(dx, dy, core):
        return {"cp": (y + dy) % ny, "tp": ((x + dx) % nx) * 2 + core}

    def flat(dx, dy, core):
        return ((y + dy) % ny) * (2 * nx) + ((x + dx) % nx) * 2 + core

    loads = [pltpu.make_async_copy(w1g_ref, vg, wsem.at[0]),
             pltpu.make_async_copy(w1u_ref, vu, wsem.at[1]),
             pltpu.make_async_copy(w2_ref, vd, wsem.at[2])]
    own = pltpu.make_async_copy(t_ref, tg_ref.at[flat(0, 0, c)], lsem.at[0])

    barrier = pltpu.get_barrier_semaphore()

    def greet(k, _):
        other = (y * 2 * nx + tp + k) % (2 * nchip)
        pl.semaphore_signal(barrier, inc=1, device_id={"cp": other // (2 * nx), "tp": other % (2 * nx)}, device_id_type=MESH)
        return 0

    lax.fori_loop(1, 2 * nchip, greet, 0)
    pl.semaphore_wait(barrier, 2 * nchip - 1)

    copies = gather_copies(ntok)

    def ici(k):
        blk, lo, n, step = copies[k]
        here = tg_ref.at[flat(blk[0], blk[1], c), pl.ds(lo, n), :]
        src = t_ref.at[pl.ds(lo, n), :] if blk == (0, 0) else here
        return pltpu.make_async_remote_copy(src_ref=src, dst_ref=here, send_sem=ag_s.at[k], recv_sem=ag_r.at[k],
                                            device_id=dev(step[0], step[1], c), device_id_type=MESH)

    def ici_in(k):
        blk, lo, n, step = copies[k]
        here = tg_ref.at[flat(blk[0] - step[0] + nx, blk[1] - step[1] + ny, c), pl.ds(lo, n), :]
        return pltpu.make_async_remote_copy(src_ref=here, dst_ref=here, send_sem=ag_s.at[k], recv_sem=ag_r.at[k],
                                            device_id=dev(nx - step[0], ny - step[1], c), device_id_type=MESH)

    def d2d(j, core):
        blk = ORDER[j]
        here = tg_ref.at[flat(blk[0], blk[1], core)]
        src = t_ref if (j == 0) else here
        return pltpu.make_async_remote_copy(src_ref=src, dst_ref=here, send_sem=dd_s.at[j], recv_sem=dd_r.at[j],
                                            device_id=dev(0, 0, 1 - c), device_id_type=MESH)

    def d2d_in(j):
        blk = ORDER[j]
        here = tg_ref.at[flat(blk[0], blk[1], 1 - c)]
        return pltpu.make_async_remote_copy(src_ref=here, dst_ref=here, send_sem=dd_s.at[j], recv_sem=dd_r.at[j],
                                            device_id=dev(0, 0, 1 - c), device_id_type=MESH)

    def round_(w):
        if w > 0:
            for k, cp in enumerate(copies):
                if dist(cp[0]) == w - 1:
                    ici_in(k).wait_recv()
        for k, cp in enumerate(copies):
            if dist(cp[0]) == w:
                ici(k).start()
        for j, b in enumerate(ORDER):
            if dist(b) == w:
                d2d(j, c).start()

    def siblings(w):
        for j, b in enumerate(ORDER):
            if dist(b) == w:
                d2d_in(j).wait_recv()

    round_(0)
    own.start()
    for l in loads:
        l.start()

    def back(j, s, slot):
        core = c if s == 0 else 1 - c
        return pltpu.make_async_remote_copy(src_ref=zb.at[slot], dst_ref=rz_ref.at[slot], send_sem=rt_s.at[slot],
                                            recv_sem=rt_r.at[slot],
                                            device_id=dev(look(DX, j), look(DY, j), core), device_id_type=MESH)

    def work(g, _):
        for w in range(1, 5):
            @pl.when(g == w - 1)
            def _():
                round_(w)
                if w == 1:
                    siblings(0)
                siblings(w)
                if w == 1:
                    own.wait()
                    for l in loads:
                        l.wait()

        def fetch(i):
            j = g * per + i // 2
            core = c if i % 2 == 0 else 1 - c
            d = flat(look(DX, j), look(DY, j), core)
            return d, pltpu.make_async_copy(tg_ref.at[d], tb.at[i % 2], tsem.at[i % 2])

        fetch(0)[1].start()
        for i in range(homes):
            d, cp = fetch(i)
            cp.wait()
            if i + 1 < homes:
                fetch(i + 1)[1].start()
            rows = lax.broadcasted_iota(jnp.int32, (2 * cap, ntok), 0)
            rank = jnp.where(rows < cap, mc_ref[0, pl.ds(d, 1), :], mc_ref[1, pl.ds(d, 1), :])
            sel = (rank == jnp.where(rows < cap, rows, rows - cap) + 1).astype(f32).astype(bf16)
            for n in range(0, dm, 512):
                got = jnp.dot(sel, tb[i % 2, :, n:n + 512], preferred_element_type=f32)
                xin[0, i * cap:(i + 1) * cap, n:n + 512] = got[:cap].astype(bf16)
                xin[1, i * cap:(i + 1) * cap, n:n + 512] = got[cap:].astype(bf16)

        for l in range(2):
            def up(at, n):
                a = jnp.dot(xin[l], vg[l, :, pl.ds(at, n)], preferred_element_type=f32)
                b = jnp.dot(xin[l], vu[l, :, pl.ds(at, n)], preferred_element_type=f32)
                act[:, pl.ds(at, n)] = (a * jax.nn.sigmoid(a) * b).astype(bf16)

            whole = ff // 256
            lax.fori_loop(0, whole, lambda n, _: (up(pl.multiple_of(n * 256, 256), 256), 0)[1], 0)
            if ff % 256:
                up(whole * 256, ff % 256)

            def down(n, _):
                at = pl.multiple_of(n * 256, 256)
                z = jnp.dot(act[...], vd[l, :, pl.ds(at, 256)], preferred_element_type=f32)
                for i in range(homes):
                    zb[g * homes + i, l * cap:(l + 1) * cap, pl.ds(at, 256)] = z[i * cap:(i + 1) * cap].astype(bf16)
                return 0

            lax.fori_loop(0, dm // 256, down, 0)

        for i in range(homes):
            j = g * per + i // 2
            if i == 0:
                @pl.when(g == 0)
                def _():
                    pltpu.make_async_copy(zb.at[0], rz_ref.at[0], lsem.at[1]).start()

                @pl.when(g > 0)
                def _():
                    back(j, 0, g * homes).start()
            else:
                back(j, i % 2, g * homes + i).start()
        return 0

    lax.fori_loop(0, groups, work, 0)

    acc_ref[...] = jnp.zeros_like(acc_ref)

    def arrived(j, s, slot):
        core = c if s == 0 else 1 - c
        return pltpu.make_async_remote_copy(src_ref=zb.at[slot], dst_ref=rz_ref.at[slot], send_sem=rt_s.at[slot],
                                            recv_sem=rt_r.at[slot],
                                            device_id=dev(nx - look(DX, j), ny - look(DY, j), core), device_id_type=MESH)

    def combine(j, _):
        @pl.when(j == 0)
        def _():
            pltpu.make_async_copy(zb.at[0], rz_ref.at[0], lsem.at[1]).wait()

        @pl.when(j > 0)
        def _():
            arrived(j, 0, 2 * j).wait_recv()

        arrived(j, 1, 2 * j + 1).wait_recv()
        pulls = [pltpu.make_async_copy(rz_ref.at[2 * j + s], zin.at[pl.ds(s * 2 * cap, 2 * cap), :], zsem.at[s]) for s in range(2)]
        for p in pulls:
            p.start()
        base = [flat(nx - look(DX, j), ny - look(DY, j), core) * (2 * cap) for core in (c, 1 - c)]
        lane = lax.broadcasted_iota(jnp.int32, (ntok, 4 * cap), 1)
        want = jnp.where(lane < 2 * cap, base[0] + lane, base[1] + lane - 2 * cap)
        g = jnp.zeros((ntok, 4 * cap), f32)
        for k in range(code_ref.shape[1]):
            g = g + jnp.where(code_ref[:, k:k + 1] == want, gate_ref[:, k:k + 1], 0.0)
        g1 = g.astype(bf16)
        rest = g - g1.astype(f32)
        g2 = rest.astype(bf16)
        g3 = (rest - g2.astype(f32)).astype(bf16)
        for p in pulls:
            p.wait()

        def col(n, _):
            at = pl.ds(pl.multiple_of(n * 512, 512), 512)
            z = zin[:, at]
            acc_ref[:, at] += (jnp.dot(g1, z, preferred_element_type=f32)
                               + (jnp.dot(g2, z, preferred_element_type=f32) + jnp.dot(g3, z, preferred_element_type=f32)))
            return 0

        lax.fori_loop(0, dm // 512, col, 0)
        return 0

    lax.fori_loop(0, nchip, combine, 0)

    for k in range(len(copies)):
        ici(k).wait_send()
    for j in range(nchip):
        d2d(j, c).wait_send()

    def drain(j, _):
        @pl.when(j > 0)
        def _():
            arrived(j, 0, 2 * j).wait_send()

        arrived(j, 1, 2 * j + 1).wait_send()
        return 0

    lax.fori_loop(0, nchip, drain, 0)


def moe(t, mc, code, gates, w1g, w1u, w2, nx, ny, cap):
    ntok, dm = t.shape
    nle, _, ff = w1g.shape
    ndev = 2 * nx * ny
    groups = 4
    rows = ndev // groups * cap
    any_ = pl.BlockSpec(memory_space=pl.ANY)
    vm = pl.BlockSpec(memory_space=pltpu.VMEM)
    ncopy = len(gather_copies(ntok))
    dma = pltpu.SemaphoreType.DMA
    return pl.pallas_call(
        functools.partial(moe_kernel, nx, ny, cap, groups),
        in_specs=[any_, vm, vm, vm, any_, any_, any_],
        out_specs=[vm, any_, any_],
        out_shape=[jax.ShapeDtypeStruct((ntok, dm), f32),
                   jax.ShapeDtypeStruct((ndev, ntok, dm), bf16),
                   jax.ShapeDtypeStruct((ndev, nle * cap, dm), bf16)],
        scratch_shapes=[pltpu.VMEM((nle, dm, ff), bf16), pltpu.VMEM((nle, dm, ff), bf16), pltpu.VMEM((nle, ff, dm), bf16),
                        pltpu.VMEM((nle, rows, dm), bf16), pltpu.VMEM((rows, ff), bf16),
                        pltpu.VMEM((ndev, nle * cap, dm), bf16), pltpu.VMEM((2, ntok, dm), bf16),
                        pltpu.VMEM((2 * nle * cap, dm), bf16),
                        dma((3,)), dma((2,)), dma((2,)), dma((2,)), dma((ncopy,)), dma((ncopy,)),
                        dma((nx * ny,)), dma((nx * ny,)), dma((ndev,)), dma((ndev,))],
        compiler_params=pltpu.CompilerParams(collective_id=0, has_side_effects=True, vmem_limit_bytes=VMEM_MAX),
        cost_estimate=pl.CostEstimate(flops=6 * ndev * nle * cap * dm * ff, bytes_accessed=10 * nle * dm * ff, transcendentals=0),
    )(t, mc, code, gates, w1g, w1u, w2)


def solution(mesh):
    ncp = mesh.shape["cp"]
    ntp = mesh.shape["tp"]
    ndev = ncp * ntp
    rows = P(("dp", "cp", "tp"), None)
    cols = P(None, "tp")
    wrows = P("tp", None)
    rep = P(None)
    exps = P(("cp", "tp"), None, None)

    def layer(x, g_attn, wq, wk, wv, wo, g_mlp, idx, gates, w1g, w1u, w2, ws1g, ws1u, ws2):
        r = lax.axis_index("cp")
        me = r * ntp + lax.axis_index("tp")
        ntok, dm = x.shape
        seq = ntok * ndev
        nloc = seq // ncp
        nle = w1g.shape[0]
        num_e = nle * ndev
        top = idx.shape[1]
        cap = -(-top * (2 * ntok // num_e + 1) // 8) * 8

        xg = lax.all_gather(rms_norm(x, g_attn), "tp", axis=0, tiled=True)
        idx_all = lax.all_gather(idx, ("cp", "tp"), axis=0, tiled=True)

        upto = (jnp.arange(ntok)[:, None] <= jnp.arange(ntok)[None, :]).astype(bf16)
        mine = me * nle + jnp.arange(nle)
        hit = jnp.any(idx_all[None] == mine[:, None, None], axis=-1).reshape(nle * ndev, ntok)
        mc = jnp.where(hit, jnp.dot(hit.astype(bf16), upto, preferred_element_type=f32), 0.0)
        mc = mc.astype(jnp.int32).reshape(nle, ndev, ntok)
        named = idx[:, :, None] == jnp.arange(num_e)[None, None, :]
        before = lax.dot_general(upto, jnp.any(named, axis=1).astype(bf16), (((0,), (0,)), ((), ())), preferred_element_type=f32) - 1.0
        rank = jnp.sum(jnp.where(named, before[:, None, :], 0.0), axis=-1).astype(jnp.int32)
        code = idx * cap + rank

        half = HEAD // 2
        pos = layout_pos(r * nloc + jnp.arange(nloc), ncp, seq)
        freq = ROPE_BASE ** (-jnp.arange(half, dtype=f32) / half)
        ang = pos.astype(f32)[:, None] * freq[None, :]
        cs, sn = jnp.cos(ang), jnp.sin(ang)
        q, kv = qkv(xg, wq, wk, wv, jnp.concatenate([cs, cs], 1), jnp.concatenate([-sn, sn], 1))
        kv_all = lax.all_gather(kv, "cp", axis=0, tiled=True)
        wo_all = lax.all_gather(wo, "tp", axis=0, tiled=True)
        ws2_all = lax.all_gather(ws2, "tp", axis=0, tiled=True)
        o = attention(q, kv_all, ncp)
        o = lax.all_to_all(o, "tp", 0, 1, tiled=True)
        attn = jnp.dot(o, wo_all, preferred_element_type=f32)
        h = (x.astype(f32) + attn).astype(bf16)
        t = rms_norm(h, g_mlp)

        routed, tg, _ = moe(t, mc, code, gates, w1g, w1u, w2, ntp // 2, ncp, cap)
        tl = lax.dynamic_slice_in_dim(tg, r * ntp, ntp, 0).reshape(nloc, dm)
        u = (jax.nn.silu(jnp.dot(tl, ws1g, preferred_element_type=f32)) * jnp.dot(tl, ws1u, preferred_element_type=f32)).astype(bf16)
        u = lax.all_to_all(u, "tp", 0, 1, tiled=True)
        shared = jnp.dot(u, ws2_all, preferred_element_type=f32)
        return (h.astype(f32) + shared + routed).astype(bf16)

    return jax.shard_map(layer, mesh=mesh,
                         in_specs=(rows, rep, cols, cols, cols, wrows, rep, rows, rows, exps, exps, exps, cols, cols, wrows),
                         out_specs=rows, check_vma=False)
```

time: 1430 us -> 652 us (0.46)
  waiting for transfers between devices: 597 us -> 139 us
  Pallas kernels: 0 us -> 399 us
  local copies, waits for them, and re-layouts: 256 us -> 19.2 us
  matrix products: 249 us -> 26 us
  blocking collectives: 157 us -> 30.4 us
  other arithmetic: 115 us -> 11.1 us
  starting transfers between devices: 33 us -> 10.2 us
    all_to_all x3 -> x2, waiting for transfers between devices: 475 us -> 42 us  [the longest x1 23.1 us: layer(): o = lax.all_to_all(o, 'tp', 0, 1, tiled=True)]
    pallas_call x0 -> x3, Pallas kernels: none -> 399 us  [the longest x1 303 us: moe(): pl.pallas_call(functools.partial(moe_kernel, nx, ny, cap, groups), in_spe...]
    dot_general x11 -> x6, matrix products: 249 us -> 26 us  [the longest x1 8.85 us: layer(): shared = jnp.dot(u, ws2_all, preferred_element_type=f32)]
    all_to_all x1 -> x0, blocking collectives: 157 us -> none  [layer(): back = lax.all_to_all(back, 'cp', 0, 0, tiled=True)]
    reshape x6 -> x1, local copies, waits for them, and re-layouts: 88 us -> 0.06 us  [layer(): jnp.any(idx_all[None] == mine[:, None, None], axis=-1)]
    all_to_all x4 -> x2, local copies, waits for them, and re-layouts: 72.4 us -> 2.52 us  [the longest x1 1.31 us: layer(): o = lax.all_to_all(o, 'tp', 0, 1, tiled=True)]
    reduce_scatter x2 -> x0, waiting for transfers between devices: 60.6 us -> none  [the longest x1 60.6 us: layer(): lax.psum_scatter(jnp.dot(o, wo, preferred_element_type=f32), 'tp', scatte...]
    reduce_sum x3 -> x1, other arithmetic: 57.6 us -> 0.06 us  [layer(): jnp.sum(jnp.where(named, before[:, None, :], 0.0), axis=-1)]
  transfers between devices with their start and end apart: 9 -> 6, of which waited for: 6 -> 4; matrix products, arithmetic and copies ran while one was open for 32% -> 6% of each run, Pallas kernels for 0% -> 60%
where the time goes in v1:
time: 652 us; the launch traced here: 648 us
  Pallas kernels  399 us (61%)
  waiting for transfers between devices  139 us (21%)
  blocking collectives  30.4 us (5%)
  matrix products  26 us (4%)
  local copies, waits for them, and re-layouts  19.2 us (3%)
  between operations  13.3 us (2%)
  other arithmetic  11.1 us (2%)
  starting transfers between devices  10.2 us (2%)
    pallas_call x1, Pallas kernels, moe(): pl.pallas_call(functools.partial(moe_kernel, nx, ny, cap, groups), in_spe...  303 us
    pallas_call x1, Pallas kernels, attention(): pl.pallas_call(functools.partial(attn_kernel, ncp, piece, bq, bk), grid=(...  85.2 us
    all_gather x1, waiting for transfers between devices, layer(): kv_all = lax.all_gather(kv, 'cp', axis=0, tiled=True)  50.1 us
    all_gather x1, waiting for transfers between devices, layer(): xg = lax.all_gather(rms_norm(x, g_attn), 'tp', axis=0, tiled=True)  45.9 us
    all_gather x1, blocking collectives, layer(): idx_all = lax.all_gather(idx, ('cp', 'tp'), axis=0, tiled=True)  30.4 us
    all_to_all x1, waiting for transfers between devices, layer(): o = lax.all_to_all(o, 'tp', 0, 1, tiled=True)  23.1 us
    all_to_all x1, waiting for transfers between devices, layer(): u = lax.all_to_all(u, 'tp', 0, 1, tiled=True)  19 us
  transfers between devices with their start and end apart: 6, of which 4 were waited for; matrix products, arithmetic and copies ran while one was open for 6% of the time, Pallas kernels for 60%

profile of v1, /device:TPU:97, one launch (start us, length us, event | category | flops | bytes accessed | tf_op | source)
XLA Modules:
  0.0 648.3 jit_solution(13768347497958713543)
XLA Ops:
  6.6 1.5 fusion.4
  8.1 2.5 fusion.6
  10.8 3.7 fusion.12
  14.5 1.7 pad_maximum_fusion
  16.2 45.9 %all-gather.5.cloned.1.call-done.x_ref = bf16[2048,2048]{1,0:T(8,128)(2,1)} async-done(((bf16[256,2048]{1,0:T(8,128)(2,1)}), bf16[2048,2048]{1,0:T(8,128)(2,1)}) %all-gather.5.cloned.1.call-update) | async-done | bytes 8388624 | tf_op jit(solution)/shard_map/all_gather | solution.py:451
  62.1 1.2 copy-done.3
  63.3 9.8 %shard_map.145 = (bf16[2048,256]{1,0:T(8,128)(2,1)S(1)}, bf16[2048,512]{1,0:T(8,128)(2,1)}) custom-call(bf16[2048,2048]{1,0:T(8,128)(2,1)} %all-gather.5.cloned.1.call-done.x_ref, bf16[2048,256]{1,0:T(8,128)(2,1)S(1)} %copy-done.1, bf16[2048,256]{1,0:T(8,128)(2,1)S(1)} %copy-done.2, bf16[2048,256]{1,0:T(8,128)(2,1)S(1)} %copy-done.3, ...), custom_call_target="tpu_custom_call" | custom-call | flops 6442450944 | bytes 14680064 | tf_op jit(solution)/shard_map/pallas_call | solution.py:56
  75.6 30.4 %all_gather.18 = s32[8192,6]{0,1:T(8,128)S(1)} all-gather(s32[256,6]{0,1:T(8,128)S(1)} %copy-done.10), channel_id=1, replica_groups=mesh['dp'=1,'cp'=4,'tp'=8] {'cp','tp'}, dimensions={0}, use_global_device_ids=true | all-gather | bytes 202752 | tf_op jit(solution)/shard_map/all_gather | solution.py:452
  106.1 50.1 %all-gather.7.cloned.1.call-done.k_ref.v_ref = bf16[8192,512]{1,0:T(8,128)(2,1)} async-done(((bf16[2048,512]{1,0:T(8,128)(2,1)}), bf16[8192,512]{1,0:T(8,128)(2,1)}) %all-gather.7.cloned.1.call-update) | async-done | bytes 8388624 | tf_op jit(solution)/shard_map/all_gather | solution.py:470
  156.2 3.4 copy-done
  159.6 85.2 %shard_map.146 = bf16[2048,256]{1,0:T(8,128)(2,1)S(1)} custom-call(bf16[2048,256]{1,0:T(8,128)(2,1)S(1)} %copy-done.5, bf16[8192,512]{1,0:T(8,128)(2,1)S(1)} %copy-done, bf16[8192,512]{1,0:T(8,128)(2,1)S(1)} %copy-done), custom_call_target="tpu_custom_call" | custom-call | flops 17179869184 | bytes 12582912 | tf_op jit(solution)/shard_map/pallas_call | solution.py:124
  244.8 1.3 copy.37
  246.1 5.2 all-to-all-start
  254.4 23.1 %all-to-all-done = bf16[8,256,256]{1,2,0:T(8,128)(2,1)S(1)} async-done(((bf16[8,256,256]{1,2,0:T(8,128)(2,1)}), bf16[8,256,256]{1,2,0:T(8,128)(2,1)S(1)}, u32[]{:S(2)}, u32[]{:S(2)}) %all-to-all-start) | async-done | bytes 1048608 | tf_op jit(solution)/shard_map/all_to_all | solution.py:474
  277.4 5.9 fusion.7
  284.3 1.3 fusion.9.t_ref
  285.6 303.5 %shard_map.147 = (f32[256,2048]{1,0:T(8,128)}, bf16[32,256,2048]{2,1,0:T(8,128)(2,1)}, bf16[32,112,2048]{2,1,0:T(8,128)(2,1)}) custom-call(bf16[256,2048]{1,0:T(8,128)(2,1)} %fusion.9.t_ref, s32[2,32,256]{2,1,0:T(8,128)} %bitcast.30, s32[256,6]{1,0:T(8,128)} %copy.39.code_ref, f32[256,6]{1,0:T(8,128)} %copy.40.gate_ref, bf16[2,2048,1408]{2,1,0:T(8,128)(2,1)} %w1g_ref.1, ...), custom_call_target="tpu_custom_call" | custom-call | flops 62008590336 | bytes 57671680 | tf_op jit(solution)/shard_map/pallas_call | solution.py:412
  589.1 8.4 %constant_dynamic-slice_fusion = bf16[8,256,2048]{2,1,0:T(8,128)(2,1)} fusion(bf16[32,256,2048]{2,1,0:T(8,128)(2,1)} %get-tuple-element.11, s32[]{:T(128)S(6)} %select_n.43), kind=kLoop, calls=%fused_computation.49 | loop fusion | bytes 16777220 | tf_op jit(solution)/shard_map/dynamic_slice | solution.py:480
  597.5 6.9 %fusion.18 = f32[2048,352]{0,1:T(8,128)S(1)} fusion(bf16[2048,2048]{1,0:T(8,128)(2,1)} %bitcast.24, bf16[2048,352]{0,1:T(8,128)(2,1)S(1)} %copy-done.13), kind=kOutput, calls=%fused_computation.50 | convolution fusion | flops 2952790016 | bytes 12713984 | tf_op jit(solution)/shard_map/dot_general | solution.py:481
  604.4 3.5 fusion
  607.9 1.2 copy.45
  609.1 4.8 all-to-all-start.1
  613.9 19.0 %all-to-all-done.1 = bf16[8,256,352]{1,2,0:T(8,128)(2,1)S(1)} async-done(((bf16[8,256,352]{1,2,0:T(8,128)(2,1)}), bf16[8,256,352]{1,2,0:T(8,128)(2,1)S(1)}, u32[]{:S(2)}, u32[]{:S(2)}) %all-to-all-start.1) | async-done | bytes 1441824 | tf_op jit(solution)/shard_map/all_to_all | solution.py:482
  632.9 8.8 %fusion.2 = bf16[256,2048]{1,0:T(8,128)(2,1)} fusion(f32[256,2048]{1,0:T(8,128)} %get-tuple-element.12, bf16[256,2816]{0,1:T(8,128)(2,1)S(1)} %bitcast.26, bf16[2816,2048]{1,0:T(8,128)(2,1)} %all-gather.11.cloned.1.call-done, bf16[256,2048]{1,0:T(8,128)(2,1)S(1)} %copy-done.8), kind=kOutput, calls=%fused_computation.9 | convolution fusion | flops 2954887168 | bytes 17170432 | tf_op jit(solution)/shard_map/dot_general | solution.py:483
  (52 shorter events, 6.6 us)
Async XLA Ops:
  6.5 55.5 %all-gather.5.cloned.1.call-start = ((), (), s32[]{:S(2)}) async-start(), calls=%async_computation.2 | async-start | bytes 9437184 | tf_op jit(solution)/shard_map/all_gather | solution.py:451
  10.6 145.6 %all-gather.7.cloned.1.call-start = ((), (), s32[]{:S(2)}) async-start(), calls=%async_computation.3 | async-start | bytes 10485760 | tf_op jit(solution)/shard_map/all_gather | solution.py:470
  14.5 47.6 %copy-start.1 = (bf16[2048,256]{1,0:T(8,128)(2,1)S(1)}, bf16[2048,256]{1,0:T(8,128)(2,1)}, u32[]{:S(2)}) copy-start(bf16[2048,256]{1,0:T(8,128)(2,1)} %wq_ref.1) | copy-start | bytes 3145732
  14.5 47.6 %copy-start.2 = (bf16[2048,256]{1,0:T(8,128)(2,1)S(1)}, bf16[2048,256]{1,0:T(8,128)(2,1)}, u32[]{:S(2)}) copy-start(bf16[2048,256]{1,0:T(8,128)(2,1)} %wk_ref.1) | copy-start | bytes 3145732
  62.1 1.2 copy-start.3
  73.1 1.0 copy-start.4
  74.1 1.5 copy-start.10
  74.1 82.1 %copy-start.5 = (bf16[2048,256]{1,0:T(8,128)(2,1)S(1)}, bf16[2048,256]{1,0:T(8,128)(2,1)}, u32[]{:S(2)}) copy-start(bf16[2048,256]{1,0:T(8,128)(2,1)} %copy-done.4) | copy-start | bytes 3145732
  74.2 180.2 %all-gather.9.cloned.1.call-start = ((), (), s32[]{:S(2)}) async-start(), calls=%async_computation.4 | async-start | bytes 9437184 | tf_op jit(solution)/shard_map/all_gather | solution.py:471
  75.0 538.9 %all-gather.11.cloned.1.call-start = ((), (), s32[]{:S(2)}) async-start(), calls=%async_computation.5 | async-start | bytes 12976128 | tf_op jit(solution)/shard_map/all_gather | solution.py:472
  156.2 3.4 copy-start
  244.8 8.0 %copy-start.12 = (f32[256,6]{0,1:T(8,128)S(1)}, f32[256,6]{0,1:T(8,128)}, u32[]{:S(2)}) copy-start(f32[256,6]{0,1:T(8,128)} %param.23) | copy-start | bytes 18436
  244.8 32.6 %copy-start.6 = (bf16[256,2048]{1,0:T(8,128)(2,1)S(1)}, bf16[256,2048]{1,0:T(8,128)(2,1)}, u32[]{:S(2)}) copy-start(bf16[256,2048]{1,0:T(8,128)(2,1)} %param.15) | copy-start | bytes 3145732
  246.1 31.3 %all-to-all-start = ((bf16[8,256,256]{1,2,0:T(8,128)(2,1)}), bf16[8,256,256]{1,2,0:T(8,128)(2,1)S(1)}, u32[]{:S(2)}, u32[]{:S(2)}) async-start(bf16[8,256,256]{1,2,0:T(8,128)(2,1)} %copy.37), calls=%async_computation | async-start | bytes 2097152 | tf_op jit(solution)/shard_map/all_to_all | solution.py:474
  277.4 6.9 %copy-start.11 = (f32[2048]{0:T(1024)S(1)}, f32[2048]{0:T(1024)}, u32[]{:S(2)}) copy-start(f32[2048]{0:T(1024)} %param.21) | copy-start | bytes 24580
  283.3 1.0 copy-start.7
  589.1 8.4 %copy-start.13 = (bf16[2048,352]{0,1:T(8,128)(2,1)S(1)}, bf16[2048,352]{0,1:T(8,128)(2,1)}, u32[]{:S(2)}) copy-start(bf16[2048,352]{0,1:T(8,128)(2,1)} %param.27) | copy-start | bytes 4325380
  597.5 6.9 %copy-start.9 = (bf16[8,256,2048]{2,1,0:T(8,128)(2,1)S(1)}, bf16[8,256,2048]{2,1,0:T(8,128)(2,1)}, u32[]{:S(2)}) copy-start(bf16[8,256,2048]{2,1,0:T(8,128)(2,1)} %constant_dynamic-slice_fusion) | copy-start | bytes 25165828
  597.5 6.9 %copy-start.14 = (bf16[2048,352]{0,1:T(8,128)(2,1)S(1)}, bf16[2048,352]{0,1:T(8,128)(2,1)}, u32[]{:S(2)}) copy-start(bf16[2048,352]{0,1:T(8,128)(2,1)} %param.28) | copy-start | bytes 4325380
  609.1 23.7 %copy-start.8 = (bf16[256,2048]{1,0:T(8,128)(2,1)S(1)}, bf16[256,2048]{1,0:T(8,128)(2,1)}, u32[]{:S(2)}) copy-start(bf16[256,2048]{1,0:T(8,128)(2,1)} %copy-done.7) | copy-start | bytes 3145732
  609.1 23.7 %all-to-all-start.1 = ((bf16[8,256,352]{1,2,0:T(8,128)(2,1)}), bf16[8,256,352]{1,2,0:T(8,128)(2,1)S(1)}, u32[]{:S(2)}, u32[]{:S(2)}) async-start(bf16[8,256,352]{1,2,0:T(8,128)(2,1)} %bitcast.28), calls=%async_computation.1 | async-start | bytes 2883584 | tf_op jit(solution)/shard_map/all_to_all | solution.py:482
Sparse Core Ops, SparseCore 0:
  10.8 51.2 all-gather.4
  74.3 81.8 all-gather.6
  157.8 48.4 all-gather.8
  207.7 71.6 all-gather.10

commit v2 on v1

v2 whole, which is shorter than its diff:
```python
import functools

import jax
import jax.numpy as jnp
from jax import lax
from jax.experimental import pallas as pl
from jax.experimental.pallas import tpu as pltpu
from jax.sharding import PartitionSpec as P

HEAD = 128
EPS = 1e-6
ROPE_BASE = 10000.0
LOG2E = 1.4426950408889634
MESH = pl.DeviceIdType.MESH
DEPTH = 3
VMEM_MAX = 66_500_000
f32 = jnp.float32
bf16 = jnp.bfloat16


def rms_norm(a, g):
    af = a.astype(f32)
    r = af * lax.rsqrt(jnp.mean(af * af, axis=-1, keepdims=True) + EPS)
    return (r * g).astype(bf16)


def layout_pos(i, ncp, seq):
    half = seq // (2 * ncp)
    r = i // (2 * half)
    w = i % (2 * half)
    return jnp.where(w < half, r * half + w, (2 * ncp - 1 - r) * half + w - half)


def attn_kernel(x_ref, g_ref, wq_ref, wk_ref, wv_ref, c_ref, s_ref, wo_ref, ws2_ref, o_ref, wo_all, ws2_all,
                xg, q_s, kvb, m_s, l_s, acc_s, xs, xr, ds, dr, ys, yr, gs, gr, gd, ge, gl):
    ntok, dm = x_ref.shape
    w = wq_ref.shape[1]
    heads = w // HEAD
    r = lax.axis_index("cp")
    tp = lax.axis_index("tp")
    ncp, nch = kvb.shape[0], kvb.shape[1]
    nx = nch // 2
    x, c = tp // 2, tp % 2
    cexp = HEAD ** -0.5 * LOG2E

    def block(dx, core):
        return ((x + dx) % nx) * 2 + core

    def to_x(dx):
        return {"tp": block(dx, c)}

    def to_y(dy):
        return {"cp": (r + dy) % ncp}

    a = x_ref[...].astype(f32)
    n = a * lax.rsqrt(jnp.mean(a * a, axis=-1, keepdims=True) + EPS)
    xg[tp] = (n * g_ref[...]).astype(bf16)

    barrier = pltpu.get_barrier_semaphore()
    for d in (to_x(1), to_x(nx - 1), to_y(1), to_y(ncp - 1), {"tp": block(0, 1 - c)}):
        pl.semaphore_signal(barrier, inc=1, device_id=d, device_id_type=MESH)
    pl.semaphore_wait(barrier, 5)

    half = ntok // 2

    def xcopy(k, incoming=False):
        step = 1 if k in (0, 2) else nx - 1
        src = 0 if k < 2 else nx - step
        lo, num = ((0, ntok), (0, ntok), (0, half), (half, half))[k]
        at = (src - step) % nx if incoming else src
        ref = xg.at[block(at, c), pl.ds(lo, num), :]
        return pltpu.make_async_remote_copy(src_ref=ref, dst_ref=ref, send_sem=xs.at[k], recv_sem=xr.at[k],
                                            device_id=to_x(nx - step if incoming else step), device_id_type=MESH)

    def sib(dx, incoming=False):
        ref = xg.at[block(dx, 1 - c if incoming else c)]
        return pltpu.make_async_remote_copy(src_ref=ref, dst_ref=ref, send_sem=ds.at[dx], recv_sem=dr.at[dx],
                                            device_id={"tp": block(0, 1 - c)}, device_id_type=MESH)

    def ycopy(dx, s, k, incoming=False):
        step = 1 if k in (0, 2) else ncp - 1
        src = 0 if k < 2 else ncp - step
        rows = kvb.shape[2]
        lo, num = ((0, rows), (0, rows), (0, rows // 2), (rows // 2, rows // 2))[k]
        at = (src - step) % ncp if incoming else src
        b = block(dx, c if s == 0 else 1 - c)
        ref = kvb.at[(r + at) % ncp, b, pl.ds(lo, num), :]
        sem = (dx * 2 + s) * 4 + k
        return pltpu.make_async_remote_copy(src_ref=ref, dst_ref=ref, send_sem=ys.at[sem], recv_sem=yr.at[sem],
                                            device_id=to_y(ncp - step if incoming else step), device_id_type=MESH)

    shards = ((wo_ref, wo_all), (ws2_ref, ws2_all))

    def wcopy(a, k, incoming=False):
        own, full = shards[a]
        num = own.shape[0]
        step = 1 if k in (0, 2) else nx - 1
        src = 0 if k < 2 else nx - step
        lo, num = ((0, num), (0, num), (0, num // 2), (num // 2, num // 2))[k]
        at = (src - step) % nx if incoming else src
        ref = full.at[block(at, c), pl.ds(lo, num), :]
        return pltpu.make_async_remote_copy(src_ref=own if k < 2 and not incoming else ref, dst_ref=ref,
                                            send_sem=gs.at[a, k], recv_sem=gr.at[a, k],
                                            device_id=to_x(nx - step if incoming else step), device_id_type=MESH)

    def wsib(a, dx, incoming=False):
        own, full = shards[a]
        ref = full.at[block(dx, 1 - c if incoming else c)]
        return pltpu.make_async_remote_copy(src_ref=own if dx == 0 and not incoming else ref, dst_ref=ref,
                                            send_sem=gd.at[a, dx], recv_sem=ge.at[a, dx],
                                            device_id={"tp": block(0, 1 - c)}, device_id_type=MESH)

    def wown(a):
        return pltpu.make_async_copy(shards[a][0], shards[a][1].at[tp], gl.at[a])

    def wstart(a):
        wcopy(a, 0).start()
        wcopy(a, 1).start()
        wsib(a, 0).start()
        wown(a).start()

    def wpass(a):
        wcopy(a, 0, True).wait_recv()
        wcopy(a, 2).start()
        wcopy(a, 1, True).wait_recv()
        wcopy(a, 3).start()
        wsib(a, nx - 1).start()
        wsib(a, 1).start()

    def wlast(a):
        wcopy(a, 2, True).wait_recv()
        wcopy(a, 3, True).wait_recv()
        wsib(a, 2).start()

    def wend(a):
        wown(a).wait()
        for k in range(4):
            wcopy(a, k).wait_send()
        for dx in range(nx):
            wsib(a, dx, True).wait_recv()
            wsib(a, dx).wait_send()

    def qkv(dx, s):
        b = block(dx, c if s == 0 else 1 - c)
        at = pl.ds(pl.multiple_of(b * ntok, ntok), ntok)
        xb = xg[b]
        cs, sn = c_ref[at, :], s_ref[at, :]

        def turned(t):
            return (t * cs + pltpu.roll(t, HEAD // 2, 1) * sn)

        k = jnp.dot(xb, wk_ref[...], preferred_element_type=f32)
        for h in range(heads):
            kvb[r, b, h * HEAD:(h + 1) * HEAD, :] = turned(k[:, h * HEAD:(h + 1) * HEAD]).T.astype(bf16)
        kvb[r, b, w:, :] = jnp.dot(xb, wv_ref[...], preferred_element_type=f32).astype(bf16)
        q = jnp.dot(xb, wq_ref[...], preferred_element_type=f32)
        for h in range(heads):
            q_s[at, h * HEAD:(h + 1) * HEAD] = turned(q[:, h * HEAD:(h + 1) * HEAD]).astype(bf16)
        ycopy(dx, s, 0).start()
        ycopy(dx, s, 1).start()

    def pass_on(dx, s):
        for k in (0, 1):
            ycopy(dx, s, k, True).wait_recv()
        for k in (2, 3):
            ycopy(dx, s, k).start()

    xcopy(0).start()
    xcopy(1).start()
    sib(0).start()
    m_s[...] = jnp.full_like(m_s, -1e30)
    l_s[...] = jnp.zeros_like(l_s)
    acc_s[...] = jnp.zeros_like(acc_s)
    qkv(0, 0)
    sib(0, True).wait_recv()
    qkv(0, 1)
    xcopy(0, True).wait_recv()
    xcopy(2).start()
    sib(nx - 1).start()
    xcopy(1, True).wait_recv()
    xcopy(3).start()
    sib(1).start()
    qkv(nx - 1, 0)
    qkv(1, 0)
    for dx in (nx - 1, 1):
        sib(dx, True).wait_recv()
        qkv(dx, 1)
    for s in (0, 1):
        pass_on(0, s)
    wstart(0)
    wstart(1)
    xcopy(2, True).wait_recv()
    xcopy(3, True).wait_recv()
    sib(2).start()
    qkv(2, 0)
    sib(2, True).wait_recv()
    qkv(2, 1)

    def attend(h, qb, rank, kb, chunks, diag):
        rows = pl.ds(pl.multiple_of(qb * ntok, ntok), ntok)
        cols = slice(h * HEAD, (h + 1) * HEAD)
        q = q_s[rows, cols]
        sc = []
        for j in range(chunks):
            t = jnp.dot(q, kvb[rank, kb + j, cols, :], preferred_element_type=f32)
            if diag and j == chunks - 1:
                t = jnp.where(lax.broadcasted_iota(jnp.int32, t.shape, 1) <= lax.broadcasted_iota(jnp.int32, t.shape, 0), t, -1e30)
            sc.append(t)
        m_old = m_s[h, rows, :]
        top = sc[0]
        for t in sc[1:]:
            top = jnp.maximum(top, t)
        m_new = jnp.maximum(m_old, jnp.max(top, axis=1, keepdims=True))
        alpha = jnp.exp2((m_old - m_new) * cexp)
        ps = [jnp.exp2((t - m_new[:, :1]) * cexp) for t in sc]
        tot = ps[0]
        for p in ps[1:]:
            tot = tot + p
        pv = None
        for j, p in enumerate(ps):
            t = jnp.dot(p.astype(bf16), kvb[rank, kb + j, w:, cols], preferred_element_type=f32)
            pv = t if pv is None else pv + t
        l_s[h, rows, :] = alpha * l_s[h, rows, :] + jnp.sum(tot, axis=1, keepdims=True)
        acc_s[h, rows, :] = alpha * acc_s[h, rows, :] + pv
        m_s[h, rows, :] = m_new

    per = nch // 2

    def full(rank, qbase, kb):
        def go(i, _):
            for h in range(heads):
                attend(h, qbase + i, rank, kb, per, False)
            return 0

        lax.fori_loop(0, per, go, 0)

    def own_diag(second, _):
        base = second * per
        for i in range(per):
            for h in range(heads):
                attend(h, base + i, r, base, i + 1, True)
        return 0

    lax.fori_loop(0, 2, own_diag, 0)
    for dx in (nx - 1, 1):
        for s in (0, 1):
            pass_on(dx, s)
    full(r, per, 0)
    for s in (0, 1):
        pass_on(2, s)
    wpass(0)

    def other(dy):
        rank = (r + dy) % ncp
        low = jnp.where(rank < r, 0, per)
        full(rank, per, 0)
        full(rank, low, low)

    other(1)
    wlast(0)
    other(ncp - 1)
    wpass(1)
    for dx in range(nx):
        for s in (0, 1):
            for k in (2, 3):
                ycopy(dx, s, k, True).wait_recv()
    other(2)
    wlast(1)
    for h in range(heads):
        o_ref[:, h * HEAD:(h + 1) * HEAD] = (acc_s[h] / l_s[h]).astype(bf16)

    wend(0)
    wend(1)
    for k in range(4):
        xcopy(k).wait_send()
    for dx in range(nx):
        sib(dx).wait_send()
        for s in (0, 1):
            for k in range(4):
                ycopy(dx, s, k).wait_send()


def attention(x, g, wq, wk, wv, cos, sin, wo, ws2, ncp, ntp):
    ntok, dm = x.shape
    w = wq.shape[1]
    heads = w // HEAD
    n = ntok * ntp
    vm = pl.BlockSpec(memory_space=pltpu.VMEM)
    any_ = pl.BlockSpec(memory_space=pl.ANY)
    dma = pltpu.SemaphoreType.DMA
    return pl.pallas_call(
        attn_kernel,
        in_specs=[vm] * 7 + [any_] * 2,
        out_specs=[vm, any_, any_],
        out_shape=[jax.ShapeDtypeStruct((n, w), bf16), jax.ShapeDtypeStruct((ntp,) + wo.shape, bf16),
                   jax.ShapeDtypeStruct((ntp,) + ws2.shape, bf16)],
        scratch_shapes=[pltpu.VMEM((ntp, ntok, dm), bf16), pltpu.VMEM((n, w), bf16), pltpu.VMEM((ncp, ntp, 2 * w, ntok), bf16),
                        pltpu.VMEM((heads, n, HEAD), f32), pltpu.VMEM((heads, n, HEAD), f32), pltpu.VMEM((heads, n, HEAD), f32),
                        dma((4,)), dma((4,)), dma((ntp // 2,)), dma((ntp // 2,)), dma((4 * ntp,)), dma((4 * ntp,)),
                        dma((2, 4)), dma((2, 4)), dma((2, ntp // 2)), dma((2, ntp // 2)), dma((2,))],
        compiler_params=pltpu.CompilerParams(collective_id=1, has_side_effects=True, vmem_limit_bytes=60 * 2**20),
        cost_estimate=pl.CostEstimate(flops=6 * n * dm * w + 2 * n * n * ncp * w, bytes_accessed=16 * n * dm, transcendentals=0),
    )(x, g.reshape(1, dm), wq, wk, wv, cos, sin, wo, ws2)


ORDER = [(0, 0), (1, 0), (3, 0), (0, 1), (0, 3), (2, 0), (0, 2), (1, 1),
         (1, 3), (3, 1), (3, 3), (2, 1), (2, 3), (1, 2), (3, 2), (2, 2)]
DIST = [0, 1, 2, 1]


def packed(values):
    return [sum(v << (2 * i) for i, v in enumerate(values[k:k + 8])) for k in (0, 8)]


DX, DY = packed([o[0] for o in ORDER]), packed([o[1] for o in ORDER])


def look(table, j):
    a, b = table
    return ((a + (j // 8) * (b - a)) >> (2 * (j % 8))) & 3


def gather_copies(rows):
    h, q = rows // 2, rows // 4
    out = []
    for flip in (False, True):
        base = h if flip else 0
        fw = (lambda a, b: (b, a)) if flip else (lambda a, b: (a, b))

        def add(rank, blk, lo, n, step):
            out.append((rank, fw(*blk), base + lo, n, fw(*step)))

        add(0, (0, 0), 0, h, (1, 0))
        add(0, (0, 0), 0, h, (3, 0))
        add(1, (3, 0), 0, q, (1, 0))
        add(1, (1, 0), q, q, (3, 0))
        for b in (3, 1, 0, 2):
            add(2, (b, 0), 0, h, (0, 1))
            add(2, (b, 0), 0, h, (0, 3))
            add(3, (b, 3), 0, q, (0, 1))
            add(3, (b, 1), q, q, (0, 3))
    out.sort(key=lambda t: t[0])
    return [t[1:] for t in out]


def send_order():
    q = {d: [(d, e, s) for e in es for s in (0, 1) if (d, e, s) != (0, 0, 0)]
         for d, es in {0: (1, 3, 2, 0), 1: (1, 3, 2, 0), 3: (3, 1, 0, 2), 2: (0, 2, 1, 3)}.items()}
    out = []
    while any(q.values()):
        for d in (1, 3, 1, 3, 2, 0, 2, 0):
            if q[d]:
                dx, dy, s = q[d].pop(0)
                out.append((ORDER.index((dx, dy)), s))
    return out


def dist(b):
    return DIST[b[0]] + DIST[b[1]]


def moe_kernel(nx, ny, cap, groups, t_ref, idx_ref, code_ref, gate_ref, w1g_ref, w1u_ref, w2_ref,
               ws1_ref, ws2_ref, acc_ref, tg_ref, rz_ref, ru_ref,
               vg, vu, vd, xin, act, zb, tb, zin, ia, mc_ref,
               wsem, tsem, zsem, lsem, ag_s, ag_r, dd_s, dd_r, rt_s, rt_r, ix_s, ix_r,
               us_s, us_r, ssem):
    ntok, dm = t_ref.shape
    ff = w1g_ref.shape[2]
    y = lax.axis_index("cp")
    tp = lax.axis_index("tp")
    x, c = tp // 2, tp % 2
    nchip = nx * ny
    per = nchip // groups
    homes = 2 * per

    def dev(dx, dy, core):
        return {"cp": (y + dy) % ny, "tp": ((x + dx) % nx) * 2 + core}

    def flat(dx, dy, core):
        return ((y + dy) % ny) * (2 * nx) + ((x + dx) % nx) * 2 + core

    def weights(l):
        return [pltpu.make_async_copy(a.at[l, pl.ds(k * (a.shape[1] // 4), a.shape[1] // 4), :],
                                      b.at[l, pl.ds(k * (a.shape[1] // 4), a.shape[1] // 4), :], wsem.at[l, n, k])
                for n, (a, b) in enumerate(((w1g_ref, vg), (w1u_ref, vu), (w2_ref, vd))) for k in range(4)]

    own = pltpu.make_async_copy(t_ref, tg_ref.at[flat(0, 0, c)], lsem.at[0])

    ia[flat(0, 0, c)] = idx_ref[...]
    barrier = pltpu.get_barrier_semaphore()

    def greet(k, _):
        other = (y * 2 * nx + tp + k) % (2 * nchip)
        pl.semaphore_signal(barrier, inc=1, device_id={"cp": other // (2 * nx), "tp": other % (2 * nx)}, device_id_type=MESH)
        return 0

    lax.fori_loop(1, 2 * nchip, greet, 0)
    pl.semaphore_wait(barrier, 2 * nchip - 1)

    copies = gather_copies(ntok)

    def ici(k):
        blk, lo, n, step = copies[k]
        here = tg_ref.at[flat(blk[0], blk[1], c), pl.ds(lo, n), :]
        src = t_ref.at[pl.ds(lo, n), :] if blk == (0, 0) else here
        return pltpu.make_async_remote_copy(src_ref=src, dst_ref=here, send_sem=ag_s.at[k], recv_sem=ag_r.at[k],
                                            device_id=dev(step[0], step[1], c), device_id_type=MESH)

    def ici_in(k):
        blk, lo, n, step = copies[k]
        here = tg_ref.at[flat(blk[0] - step[0] + nx, blk[1] - step[1] + ny, c), pl.ds(lo, n), :]
        return pltpu.make_async_remote_copy(src_ref=here, dst_ref=here, send_sem=ag_s.at[k], recv_sem=ag_r.at[k],
                                            device_id=dev(nx - step[0], ny - step[1], c), device_id_type=MESH)

    def d2d(j, core):
        blk = ORDER[j]
        here = tg_ref.at[flat(blk[0], blk[1], core)]
        src = t_ref if (j == 0) else here
        return pltpu.make_async_remote_copy(src_ref=src, dst_ref=here, send_sem=dd_s.at[j], recv_sem=dd_r.at[j],
                                            device_id=dev(0, 0, 1 - c), device_id_type=MESH)

    def d2d_in(j):
        blk = ORDER[j]
        here = tg_ref.at[flat(blk[0], blk[1], 1 - c)]
        return pltpu.make_async_remote_copy(src_ref=here, dst_ref=here, send_sem=dd_s.at[j], recv_sem=dd_r.at[j],
                                            device_id=dev(0, 0, 1 - c), device_id_type=MESH)

    def round_(w):
        h = ntok // 2
        if w == 0:
            for k, cp in enumerate(copies):
                if cp[0] == (0, 0):
                    ici(k).start()
            d2d(0, c).start()
            return
        left = {}
        into = [(k, ((cp[0][0] - cp[3][0]) % nx, (cp[0][1] - cp[3][1]) % ny), cp) for k, cp in enumerate(copies) if dist(cp[0]) == w - 1]
        for k, blk, cp in into:
            part = (blk, cp[1] // h)
            left[part] = left.get(part, 0) + cp[2]
        done = {}
        for k, blk, cp in into:
            ici_in(k).wait_recv()
            part = (blk, cp[1] // h)
            left[part] -= cp[2]
            if left[part] == 0:
                for n, out in enumerate(copies):
                    if out[0] == blk and out[1] // h == part[1]:
                        ici(n).start()
                done[blk] = done.get(blk, 0) + 1
                if done[blk] == 2:
                    d2d(ORDER.index(blk), c).start()

    def siblings(w):
        for j, b in enumerate(ORDER):
            if dist(b) == w:
                d2d_in(j).wait_recv()

    def choices(j, s, incoming=False):
        core = c if s == 0 else 1 - c
        dx, dy = look(DX, j), look(DY, j)
        ref = ia.at[flat(nx - dx, ny - dy, core) if incoming else flat(0, 0, c)]
        return pltpu.make_async_remote_copy(src_ref=ref, dst_ref=ref, send_sem=ix_s.at[2 * j + s], recv_sem=ix_r.at[2 * j + s],
                                            device_id=dev(nx - dx, ny - dy, core) if incoming else dev(dx, dy, core),
                                            device_id_type=MESH)

    def each_other(do):
        def go(j, _):
            @pl.when(j > 0)
            def _():
                do(j, 0)

            do(j, 1)
            return 0

        lax.fori_loop(0, nchip, go, 0)

    each_other(lambda j, s: choices(j, s).start())
    round_(0)
    own.start()
    for l in range(2):
        for p in weights(l):
            p.start()

    def back(j, s, slot):
        core = c if s == 0 else 1 - c
        return pltpu.make_async_remote_copy(src_ref=zb.at[slot], dst_ref=rz_ref.at[slot], send_sem=rt_s.at[slot],
                                            recv_sem=rt_r.at[slot],
                                            device_id=dev(look(DX, j), look(DY, j), core), device_id_type=MESH)

    wide = ws1_ref.shape[1] // 2
    deep = ws2_ref.shape[1]

    def ublock(i):
        return xin.at[i // nx, pl.ds(0, ntok), pl.ds((i % nx) * wide, wide)]

    def ucopy(i, incoming=False):
        dx, core = i // 2, c if i % 2 == 0 else 1 - c
        return pltpu.make_async_remote_copy(src_ref=ublock(i), dst_ref=ru_ref.at[i], send_sem=us_s.at[i], recv_sem=us_r.at[i],
                                            device_id=dev(nx - dx if incoming else dx, 0, core), device_id_type=MESH)

    def uown():
        return pltpu.make_async_copy(ublock(0), ru_ref.at[0], us_s.at[0])

    def ws2_load(i):
        j = ((x + nx - i // 2) % nx) * 2 + (c if i % 2 == 0 else 1 - c)
        return pltpu.make_async_copy(ws2_ref.at[j], vd.at[i // nx, pl.ds((i % nx) * deep, deep), :], ssem.at[1 + i])

    def shared_up():
        first = pltpu.make_async_copy(ws1_ref, vg.at[0, :, pl.ds(0, 2 * wide)], ssem.at[0])
        first.start()

        def rows_of(i):
            d = flat(i // 2, 0, c if i % 2 == 0 else 1 - c)
            return pltpu.make_async_copy(tg_ref.at[d], tb.at[i % DEPTH], tsem.at[i % DEPTH])

        for i in range(DEPTH - 1):
            rows_of(i).start()
        for i in range(2 * nx):
            ws2_load(i).start()
        first.wait()
        for i in range(2 * nx):
            rows_of(i).wait()
            if i + DEPTH - 1 < 2 * nx:
                rows_of(i + DEPTH - 1).start()
            a = jnp.dot(tb[i % DEPTH], vg[0, :, :wide], preferred_element_type=f32)
            b = jnp.dot(tb[i % DEPTH], vg[0, :, wide:2 * wide], preferred_element_type=f32)
            xin[i // nx, :ntok, (i % nx) * wide:(i % nx + 1) * wide] = (a * jax.nn.sigmoid(a) * b).astype(bf16)
        uown().start()
        for i in range(1, 2 * nx):
            ucopy(i).start()

    def shared_down():
        uown().wait()
        pulls = []
        for i in range(2 * nx):
            if i:
                ucopy(i, True).wait_recv()
            p = pltpu.make_async_copy(ru_ref.at[i], tb.at[i // nx, :, pl.ds((i % nx) * wide, wide)], ssem.at[9 + i])
            p.start()
            pulls.append(p)
        for i in range(2 * nx):
            ws2_load(i).wait()
            pulls[i].wait()

        def col(n, _):
            at = pl.ds(pl.multiple_of(n * 256, 256), 256)
            tot = acc_ref[:, at]
            for i in range(2 * nx):
                tot = tot + jnp.dot(tb[i // nx, :, (i % nx) * wide:(i % nx) * wide + deep],
                                    vd[i // nx, (i % nx) * deep:(i % nx + 1) * deep, at], preferred_element_type=f32)
            acc_ref[:, at] = tot
            return 0

        lax.fori_loop(0, dm // 256, col, 0)

    def work(g, _):
        for w in range(1, 5):
            @pl.when(g == w - 1)
            def _():
                round_(w)
                if w == 1:
                    siblings(0)
                siblings(w)
                if w == 1:
                    own.wait()
                    each_other(lambda j, s: choices(j, s, True).wait_recv())
                    upto = (lax.broadcasted_iota(jnp.int32, (ntok, ntok), 0)
                            <= lax.broadcasted_iota(jnp.int32, (ntok, ntok), 1)).astype(f32).astype(bf16)
                    for l in range(2):
                        e = (y * 2 * nx + tp) * 2 + l
                        hit = jnp.zeros((2 * nchip, ntok), jnp.bool_)
                        for k in range(code_ref.shape[1]):
                            hit = hit | (ia[:, k, :] == e)
                        hit = hit.astype(f32)
                        cum = jnp.dot(hit.astype(bf16), upto, preferred_element_type=f32)
                        mc_ref[l] = (hit * cum).astype(jnp.int32)

        def fetch(i):
            j = g * per + i // 2
            core = c if i % 2 == 0 else 1 - c
            d = flat(look(DX, j), look(DY, j), core)
            return d, pltpu.make_async_copy(tg_ref.at[d], tb.at[i % DEPTH], tsem.at[i % DEPTH])

        for i in range(DEPTH - 1):
            fetch(i)[1].start()
        for i in range(homes):
            d, cp = fetch(i)
            cp.wait()
            if i + DEPTH - 1 < homes:
                fetch(i + DEPTH - 1)[1].start()
            rows = lax.broadcasted_iota(jnp.int32, (2 * cap, ntok), 0)
            rank = jnp.where(rows < cap, mc_ref[0, pl.ds(d, 1), :], mc_ref[1, pl.ds(d, 1), :])
            sel = (rank == jnp.where(rows < cap, rows, rows - cap) + 1).astype(f32).astype(bf16)
            for n in range(0, dm, 512):
                got = jnp.dot(sel, tb[i % DEPTH, :, n:n + 512], preferred_element_type=f32)
                xin[0, i * cap:(i + 1) * cap, n:n + 512] = got[:cap].astype(bf16)
                xin[1, i * cap:(i + 1) * cap, n:n + 512] = got[cap:].astype(bf16)

        for l in range(2):
            @pl.when(g == 0)
            def _():
                for p in weights(l):
                    p.wait()

            def up(at, n):
                a = jnp.dot(xin[l], vg[l, :, pl.ds(at, n)], preferred_element_type=f32)
                b = jnp.dot(xin[l], vu[l, :, pl.ds(at, n)], preferred_element_type=f32)
                act[:, pl.ds(at, n)] = (a * jax.nn.sigmoid(a) * b).astype(bf16)

            whole = ff // 256
            lax.fori_loop(0, whole, lambda n, _: (up(pl.multiple_of(n * 256, 256), 256), 0)[1], 0)
            if ff % 256:
                up(whole * 256, ff % 256)

            def down(n, _):
                at = pl.multiple_of(n * 256, 256)
                z = jnp.dot(act[...], vd[l, :, pl.ds(at, 256)], preferred_element_type=f32)
                for i in range(homes):
                    zb[g * homes + i, l * cap:(l + 1) * cap, pl.ds(at, 256)] = z[i * cap:(i + 1) * cap].astype(bf16)
                return 0

            lax.fori_loop(0, dm // 256, down, 0)

        @pl.when(g == 0)
        def _():
            pltpu.make_async_copy(zb.at[0], rz_ref.at[0], lsem.at[1]).start()

        @pl.when(g == groups - 2)
        def _():
            for j, s in send_order():
                if j < nchip - per:
                    back(j, s, 2 * j + s).start()

        @pl.when(g == groups - 1)
        def _():
            shared_up()
            for j, s in send_order():
                if j >= nchip - per:
                    back(j, s, 2 * j + s).start()

        return 0

    lax.fori_loop(0, groups, work, 0)

    acc_ref[...] = jnp.zeros_like(acc_ref)

    def arrived(j, s, slot):
        core = c if s == 0 else 1 - c
        return pltpu.make_async_remote_copy(src_ref=zb.at[slot], dst_ref=rz_ref.at[slot], send_sem=rt_s.at[slot],
                                            recv_sem=rt_r.at[slot],
                                            device_id=dev(nx - look(DX, j), ny - look(DY, j), core), device_id_type=MESH)

    def combine(j, _):
        @pl.when(j == nchip - per)
        def _():
            shared_down()

        @pl.when(j == 0)
        def _():
            pltpu.make_async_copy(zb.at[0], rz_ref.at[0], lsem.at[1]).wait()

        @pl.when(j > 0)
        def _():
            arrived(j, 0, 2 * j).wait_recv()

        arrived(j, 1, 2 * j + 1).wait_recv()
        pulls = [pltpu.make_async_copy(rz_ref.at[2 * j + s], zin.at[pl.ds(s * 2 * cap, 2 * cap), :], zsem.at[s]) for s in range(2)]
        for p in pulls:
            p.start()
        base = [flat(nx - look(DX, j), ny - look(DY, j), core) * (2 * cap) for core in (c, 1 - c)]
        lane = lax.broadcasted_iota(jnp.int32, (ntok, 4 * cap), 1)
        want = jnp.where(lane < 2 * cap, base[0] + lane, base[1] + lane - 2 * cap)
        g = jnp.zeros((ntok, 4 * cap), f32)
        for k in range(code_ref.shape[1]):
            g = g + jnp.where(code_ref[:, k:k + 1] == want, gate_ref[:, k:k + 1], 0.0)
        g1 = g.astype(bf16)
        rest = g - g1.astype(f32)
        g2 = rest.astype(bf16)
        g3 = (rest - g2.astype(f32)).astype(bf16)
        for p in pulls:
            p.wait()

        def col(n, _):
            at = pl.ds(pl.multiple_of(n * 512, 512), 512)
            z = zin[:, at]
            acc_ref[:, at] += (jnp.dot(g1, z, preferred_element_type=f32)
                               + (jnp.dot(g2, z, preferred_element_type=f32) + jnp.dot(g3, z, preferred_element_type=f32)))
            return 0

        lax.fori_loop(0, dm // 512, col, 0)
        return 0

    lax.fori_loop(0, nchip, combine, 0)

    for k in range(len(copies)):
        ici(k).wait_send()
    for j in range(nchip):
        d2d(j, c).wait_send()

    def drain(j, s):
        arrived(j, s, 2 * j + s).wait_send()
        choices(j, s).wait_send()

    each_other(drain)
    for i in range(1, 2 * nx):
        ucopy(i).wait_send()


def moe(t, idx, code, gates, w1g, w1u, w2, ws1, ws2, nx, ny, cap):
    ntok, dm = t.shape
    nle, _, ff = w1g.shape
    ndev = 2 * nx * ny
    groups = 4
    rows = ndev // groups * cap
    any_ = pl.BlockSpec(memory_space=pl.ANY)
    vm = pl.BlockSpec(memory_space=pltpu.VMEM)
    ncopy = len(gather_copies(ntok))
    dma = pltpu.SemaphoreType.DMA
    return pl.pallas_call(
        functools.partial(moe_kernel, nx, ny, cap, groups),
        in_specs=[vm, vm, vm, vm] + [any_] * 5,
        out_specs=[vm, any_, any_, any_],
        out_shape=[jax.ShapeDtypeStruct((ntok, dm), f32),
                   jax.ShapeDtypeStruct((ndev, ntok, dm), bf16),
                   jax.ShapeDtypeStruct((ndev, nle * cap, dm), bf16),
                   jax.ShapeDtypeStruct((2 * nx, ntok, ws1.shape[1] // 2), bf16)],
        scratch_shapes=[pltpu.VMEM((nle, dm, ff), bf16), pltpu.VMEM((nle, dm, ff), bf16), pltpu.VMEM((nle, ff, dm), bf16),
                        pltpu.VMEM((nle, rows, dm), bf16), pltpu.VMEM((rows, ff), bf16),
                        pltpu.VMEM((ndev, nle * cap, dm), bf16), pltpu.VMEM((DEPTH, ntok, dm), bf16),
                        pltpu.VMEM((2 * nle * cap, dm), bf16), pltpu.VMEM((ndev,) + idx.shape, jnp.int32),
                        pltpu.VMEM((nle, ndev, ntok), jnp.int32),
                        dma((2, 3, 4)), dma((DEPTH,)), dma((2,)), dma((2,)), dma((ncopy,)), dma((ncopy,)),
                        dma((nx * ny,)), dma((nx * ny,)), dma((ndev,)), dma((ndev,)), dma((ndev,)), dma((ndev,)),
                        dma((2 * nx,)), dma((2 * nx,)), dma((17,))],
        compiler_params=pltpu.CompilerParams(collective_id=0, has_side_effects=True, vmem_limit_bytes=VMEM_MAX),
        cost_estimate=pl.CostEstimate(flops=6 * ndev * nle * cap * dm * ff, bytes_accessed=10 * nle * dm * ff, transcendentals=0),
    )(t, idx, code, gates, w1g, w1u, w2, ws1, ws2)


def solution(mesh):
    ncp = mesh.shape["cp"]
    ntp = mesh.shape["tp"]
    ndev = ncp * ntp
    rows = P(("dp", "cp", "tp"), None)
    cols = P(None, "tp")
    wrows = P("tp", None)
    rep = P(None)
    exps = P(("cp", "tp"), None, None)

    def layer(x, g_attn, wq, wk, wv, wo, g_mlp, idx, gates, w1g, w1u, w2, ws1g, ws1u, ws2):
        r = lax.axis_index("cp")
        me = r * ntp + lax.axis_index("tp")
        ntok, dm = x.shape
        seq = ntok * ndev
        nloc = seq // ncp
        nle = w1g.shape[0]
        num_e = nle * ndev
        top = idx.shape[1]
        cap = -(-top * (2 * ntok // num_e + 1) // 8) * 8

        upto = (jnp.arange(ntok)[:, None] <= jnp.arange(ntok)[None, :]).astype(bf16)
        named = idx[:, :, None] == jnp.arange(num_e)[None, None, :]
        before = lax.dot_general(upto, jnp.any(named, axis=1).astype(bf16), (((0,), (0,)), ((), ())), preferred_element_type=f32) - 1.0
        rank = jnp.sum(jnp.where(named, before[:, None, :], 0.0), axis=-1).astype(jnp.int32)
        code = idx * cap + rank

        half = HEAD // 2
        pos = layout_pos(r * nloc + jnp.arange(nloc), ncp, seq)
        freq = ROPE_BASE ** (-jnp.arange(half, dtype=f32) / half)
        ang = pos.astype(f32)[:, None] * freq[None, :]
        cs, sn = jnp.cos(ang), jnp.sin(ang)
        o, wo_all, ws2_all = attention(x, g_attn, wq, wk, wv, jnp.concatenate([cs, cs], 1), jnp.concatenate([-sn, sn], 1), wo, ws2, ncp, ntp)
        o = lax.all_to_all(o, "tp", 0, 1, tiled=True)
        attn = jnp.dot(o, wo_all.reshape(-1, dm), preferred_element_type=f32)
        h = (x.astype(f32) + attn).astype(bf16)
        t = rms_norm(h, g_mlp)

        idx_t = jnp.pad(idx.T, ((0, 8 - top), (0, 0)), constant_values=-1)
        pad = ((0, 0), (0, -ws1g.shape[1] % 128))
        ws1 = jnp.concatenate([jnp.pad(ws1g, pad), jnp.pad(ws1u, pad)], axis=1)
        added = moe(t, idx_t, code, gates, w1g, w1u, w2, ws1, ws2_all, ntp // 2, ncp, cap)[0]
        return (h.astype(f32) + added).astype(bf16)

    return jax.shard_map(layer, mesh=mesh,
                         in_specs=(rows, rep, cols, cols, cols, wrows, rep, rows, rows, exps, exps, exps, cols, cols, wrows),
                         out_specs=rows, check_vma=False)
```

time: 652 us -> 544 us (0.83)
  waiting for transfers between devices: 139 us -> 7.95 us
  Pallas kernels: 399 us -> 497 us
  blocking collectives: 30.4 us -> 0 us
  matrix products: 26 us -> 6.56 us
  local copies, waits for them, and re-layouts: 19.2 us -> 5.85 us
  between operations: 13.3 us -> 0.3 us
    all_gather x4 -> x0, waiting for transfers between devices: 96 us -> none  [the longest x1 50.1 us: layer(): kv_all = lax.all_gather(kv, 'cp', axis=0, tiled=True)]
    pallas_call x2 -> x1, Pallas kernels: 95.1 us -> 145 us  [attention(): pl.pallas_call(attn_kernel, in_specs=[vm] * 7 + [any_] * 2, out_specs=[vm...]
    pallas_call x1, Pallas kernels: 303 us -> 352 us  [moe(): pl.pallas_call(functools.partial(moe_kernel, nx, ny, cap, groups), in_spe...]
    all_gather x1 -> x0, blocking collectives: 30.4 us -> none  [layer(): idx_all = lax.all_gather(idx, ('cp', 'tp'), axis=0, tiled=True)]
    dot_general x5 -> x1, matrix products: 25.9 us -> 6.41 us  [layer(): attn = jnp.dot(o, wo_all.reshape(-1, dm), preferred_element_type=f32)]
    all_to_all x1 -> x0, waiting for transfers between devices: 19 us -> none  [layer(): u = lax.all_to_all(u, 'tp', 0, 1, tiled=True)]
    all_to_all x1, waiting for transfers between devices: 23.1 us -> 7.95 us  [layer(): o = lax.all_to_all(o, 'tp', 0, 1, tiled=True)]
    dynamic_slice x1 -> x0, local copies, waits for them, and re-layouts: 8.4 us -> none  [layer(): tl = lax.dynamic_slice_in_dim(tg, r * ntp, ntp, 0).reshape(nloc, dm)]
  transfers between devices with their start and end apart: 6 -> 1, of which waited for: 4 -> 1; matrix products, arithmetic and copies ran while one was open for 6% -> 1% of each run, Pallas kernels for 60% -> 0%
where the time goes in v2:
time: 544 us; the launch traced here: 534 us
  Pallas kernels  497 us (91%)
  other arithmetic  12 us (2%)
  waiting for transfers between devices  7.95 us (1%)
  matrix products  6.56 us (1%)
  local copies, waits for them, and re-layouts  5.85 us (1%)
    pallas_call x1, Pallas kernels, moe(): pl.pallas_call(functools.partial(moe_kernel, nx, ny, cap, groups), in_spe...  352 us
    pallas_call x1, Pallas kernels, attention(): pl.pallas_call(attn_kernel, in_specs=[vm] * 7 + [any_] * 2, out_specs=[vm...  145 us
  transfers between devices with their start and end apart: 1, of which 1 were waited for; matrix products, arithmetic and copies ran while one was open for 1% of the time, Pallas kernels for 0%

profile of v2, /device:TPU:97, one launch (start us, length us, event | category | flops | bytes accessed | tf_op | source)
XLA Modules:
  0.0 534.3 jit_solution(7382347184260886350)
XLA Ops:
  0.0 3.7 fusion.11
  3.8 1.9 pad_maximum_fusion
  5.7 144.9 %shard_map.145 = (bf16[2048,256]{1,0:T(8,128)(2,1)}, bf16[8,256,2048]{2,1,0:T(8,128)(2,1)}, bf16[8,352,2048]{2,1,0:T(8,128)(2,1)}) custom-call(bf16[256,2048]{1,0:T(8,128)(2,1)} %x_ref.1, f32[1,2048]{1,0:T(1,128)} %bitcast.18, bf16[2048,256]{1,0:T(8,128)(2,1)} %wq_ref.1, bf16[2048,256]{1,0:T(8,128)(2,1)} %wk_ref.1, bf16[2048,256]{1,0:T(8,128)(2,1)} %wv_ref.1, ...), custom_call_target="tpu_custom_call" | custom-call | flops 15032385536 | bytes 67108864 | tf_op jit(solution)/shard_map/pallas_call | solution.py:291
  150.6 0.0 copy-start.2
  150.6 0.0 copy-start.4
  150.6 0.0 copy-start.1
  150.6 4.5 all-to-all-start
  155.1 0.0 copy-done.2
  155.1 0.2 convolution_add_fusion
  155.3 0.1 select_reduce_fusion
  155.4 0.8 copy.31.code_ref
  156.2 0.0 copy-done.4
  156.2 0.8 copy.32.gate_ref
  157.0 0.8 copy.29
  157.8 1.9 copy.30
  159.7 0.6 pad.11.idx_ref
  160.3 1.8 fusion.2.ws1_ref
  162.1 8.0 %all-to-all-done = bf16[8,256,256]{2,1,0:T(8,128)(2,1)} async-done(((bf16[8,256,256]{2,1,0:T(8,128)(2,1)}), bf16[8,256,256]{2,1,0:T(8,128)(2,1)}, u32[]{:S(2)}, u32[]{:S(2)}) %all-to-all-start) | async-done | bytes 1048608 | tf_op jit(solution)/shard_map/all_to_all | solution.py:774
  170.0 6.4 %fusion.5 = (f32[256]{0:T(256)S(1)}, bf16[256,2048]{1,0:T(8,128)(2,1)S(1)}) fusion(bf16[8,256,2048]{2,1,0:T(8,128)(2,1)} %get-tuple-element.10, bf16[8,256,256]{2,1,0:T(8,128)(2,1)} %all-to-all-done, bf16[256,2048]{1,0:T(8,128)(2,1)} %x_ref.1), kind=kOutput, calls=%fused_computation.11 | convolution fusion | flops 2150629120 | bytes 11535360 | tf_op jit(solution)/shard_map/dot_general | solution.py:775
  176.5 0.9 copy-done
  177.4 0.0 copy-done.3
  177.4 1.3 fusion.7.t_ref
  178.7 352.3 %shard_map.146 = (f32[256,2048]{1,0:T(8,128)}, bf16[32,256,2048]{2,1,0:T(8,128)(2,1)}, bf16[32,112,2048]{2,1,0:T(8,128)(2,1)}, bf16[8,256,384]{2,1,0:T(8,128)(2,1)}) custom-call(bf16[256,2048]{1,0:T(8,128)(2,1)} %fusion.7.t_ref, s32[8,256]{1,0:T(8,128)} %pad.11.idx_ref, s32[256,6]{1,0:T(8,128)} %copy.31.code_ref, f32[256,6]{1,0:T(8,128)} %copy.32.gate_ref, ...), custom_call_target="tpu_custom_call" | custom-call | flops 62008590336 | bytes 57671680 | tf_op jit(solution)/shard_map/pallas_call | solution.py:720
  531.0 3.1 fusion.8
  (8 shorter events, 0.1 us)
Async XLA Ops:
  150.6 4.5 copy-start.2
  150.6 5.6 %copy-start.4 = (f32[256,6]{0,1:T(8,128)S(1)}, f32[256,6]{0,1:T(8,128)}, u32[]{:S(2)}) copy-start(f32[256,6]{0,1:T(8,128)} %param.23) | copy-start | bytes 18436
  150.6 6.4 %copy-start.1 = (bf16[2048,352]{0,1:T(8,128)(2,1)S(1)}, bf16[2048,352]{0,1:T(8,128)(2,1)}, u32[]{:S(2)}) copy-start(bf16[2048,352]{0,1:T(8,128)(2,1)} %param.27) | copy-start | bytes 4325380
  150.6 19.4 %all-to-all-start = ((bf16[8,256,256]{2,1,0:T(8,128)(2,1)}), bf16[8,256,256]{2,1,0:T(8,128)(2,1)}, u32[]{:S(2)}, u32[]{:S(2)}) async-start(bf16[8,256,256]{2,1,0:T(8,128)(2,1)} %bitcast.16), calls=%async_computation | async-start | bytes 2097152 | tf_op jit(solution)/shard_map/all_to_all | solution.py:774
  170.0 7.4 %copy-start.3 = (f32[2048]{0:T(1024)S(1)}, f32[2048]{0:T(1024)}, u32[]{:S(2)}) copy-start(f32[2048]{0:T(1024)} %param.21) | copy-start | bytes 24580
  176.4 1.0 copy-start

commit v3 on v2

v3 whole, which is shorter than its diff:
```python
import functools

import jax
import jax.numpy as jnp
from jax import lax
from jax.experimental import pallas as pl
from jax.experimental.pallas import tpu as pltpu
from jax.sharding import PartitionSpec as P

HEAD = 128
EPS = 1e-6
ROPE_BASE = 10000.0
LOG2E = 1.4426950408889634
MESH = pl.DeviceIdType.MESH
DEPTH = 3
VMEM_MAX = 66_500_000
ONE = 1
TWO = 2
f32 = jnp.float32
bf16 = jnp.bfloat16


def rms_norm(a, g):
    af = a.astype(f32)
    r = af * lax.rsqrt(jnp.mean(af * af, axis=-1, keepdims=True) + EPS)
    return (r * g).astype(bf16)


def layout_pos(i, ncp, seq):
    half = seq // (2 * ncp)
    r = i // (2 * half)
    w = i % (2 * half)
    return jnp.where(w < half, r * half + w, (2 * ncp - 1 - r) * half + w - half)


def attn_kernel(x_ref, g_ref, wq_ref, wk_ref, wv_ref, c_ref, s_ref, wo_ref, ws2_ref, o_ref, wo_all, ws2_all,
                xg, q_s, kvb, m_s, l_s, acc_s, xs, xr, ds, dr, ys, yr, gs, gr, gd, ge, gl):
    ntok, dm = x_ref.shape
    w = wq_ref.shape[ONE]
    heads = w // HEAD
    r = lax.axis_index("cp")
    tp = lax.axis_index("tp")
    ncp, nch = kvb.shape[0], kvb.shape[ONE]
    nx = nch // TWO
    x, c = tp // TWO, tp % TWO
    cexp = HEAD ** -0.5 * LOG2E

    def block(dx, core):
        return ((x + dx) % nx) * TWO + core

    def to_x(dx):
        return {"tp": block(dx, c)}

    def to_y(dy):
        return {"cp": (r + dy) % ncp}

    a = x_ref[...].astype(f32)
    n = a * lax.rsqrt(jnp.mean(a * a, axis=-ONE, keepdims=True) + EPS)
    xg[tp] = (n * g_ref[...]).astype(bf16)

    barrier = pltpu.get_barrier_semaphore()
    for d in (to_x(ONE), to_x(nx - ONE), to_y(ONE), to_y(ncp - ONE), {"tp": block(0, ONE - c)}):
        pl.semaphore_signal(barrier, inc=ONE, device_id=d, device_id_type=MESH)
    pl.semaphore_wait(barrier, 5)

    half = ntok // TWO

    def xcopy(k, incoming=False):
        step = ONE if k in (0, TWO) else nx - ONE
        src = 0 if k < TWO else nx - step
        lo, num = ((0, ntok), (0, ntok), (0, half), (half, half))[k]
        at = (src - step) % nx if incoming else src
        ref = xg.at[block(at, c), pl.ds(lo, num), :]
        return pltpu.make_async_remote_copy(src_ref=ref, dst_ref=ref, send_sem=xs.at[k], recv_sem=xr.at[k],
                                            device_id=to_x(nx - step if incoming else step), device_id_type=MESH)

    def sib(dx, incoming=False):
        ref = xg.at[block(dx, ONE - c if incoming else c)]
        return pltpu.make_async_remote_copy(src_ref=ref, dst_ref=ref, send_sem=ds.at[dx], recv_sem=dr.at[dx],
                                            device_id={"tp": block(0, ONE - c)}, device_id_type=MESH)

    def ycopy(dx, s, k, incoming=False):
        step = ONE if k in (0, TWO) else ncp - ONE
        src = 0 if k < TWO else ncp - step
        rows = kvb.shape[TWO]
        lo, num = ((0, rows), (0, rows), (0, rows // TWO), (rows // TWO, rows // TWO))[k]
        at = (src - step) % ncp if incoming else src
        b = block(dx, c if s == 0 else ONE - c)
        ref = kvb.at[(r + at) % ncp, b, pl.ds(lo, num), :]
        sem = (dx * TWO + s) * 4 + k
        return pltpu.make_async_remote_copy(src_ref=ref, dst_ref=ref, send_sem=ys.at[sem], recv_sem=yr.at[sem],
                                            device_id=to_y(ncp - step if incoming else step), device_id_type=MESH)

    shards = ((wo_ref, wo_all), (ws2_ref, ws2_all))

    def wcopy(a, k, incoming=False):
        own, full = shards[a]
        num = own.shape[0]
        step = ONE if k in (0, TWO) else nx - ONE
        src = 0 if k < TWO else nx - step
        lo, num = ((0, num), (0, num), (0, num // TWO), (num // TWO, num // TWO))[k]
        at = (src - step) % nx if incoming else src
        ref = full.at[block(at, c), pl.ds(lo, num), :]
        return pltpu.make_async_remote_copy(src_ref=own if k < TWO and not incoming else ref, dst_ref=ref,
                                            send_sem=gs.at[a, k], recv_sem=gr.at[a, k],
                                            device_id=to_x(nx - step if incoming else step), device_id_type=MESH)

    def wsib(a, dx, incoming=False):
        own, full = shards[a]
        ref = full.at[block(dx, ONE - c if incoming else c)]
        return pltpu.make_async_remote_copy(src_ref=own if dx == 0 and not incoming else ref, dst_ref=ref,
                                            send_sem=gd.at[a, dx], recv_sem=ge.at[a, dx],
                                            device_id={"tp": block(0, ONE - c)}, device_id_type=MESH)

    def wown(a):
        return pltpu.make_async_copy(shards[a][0], shards[a][ONE].at[tp], gl.at[a])

    def wstart(a):
        wcopy(a, 0).start()
        wcopy(a, ONE).start()
        wsib(a, 0).start()
        wown(a).start()

    def wpass(a):
        wcopy(a, 0, True).wait_recv()
        wcopy(a, TWO).start()
        wcopy(a, ONE, True).wait_recv()
        wcopy(a, 3).start()
        wsib(a, nx - ONE).start()
        wsib(a, ONE).start()

    def wlast(a):
        wcopy(a, TWO, True).wait_recv()
        wcopy(a, 3, True).wait_recv()
        wsib(a, TWO).start()

    def wend(a):
        wown(a).wait()
        for k in range(4):
            wcopy(a, k).wait_send()
        for dx in range(nx):
            wsib(a, dx, True).wait_recv()
            wsib(a, dx).wait_send()

    def qkv(dx, s):
        b = block(dx, c if s == 0 else ONE - c)
        at = pl.ds(pl.multiple_of(b * ntok, ntok), ntok)
        xb = xg[b]
        cs, sn = c_ref[at, :], s_ref[at, :]

        def turned(t):
            return (t * cs + pltpu.roll(t, HEAD // TWO, ONE) * sn)

        k = jnp.dot(xb, wk_ref[...], preferred_element_type=f32)
        for h in range(heads):
            kvb[r, b, h * HEAD:(h + ONE) * HEAD, :] = turned(k[:, h * HEAD:(h + ONE) * HEAD]).T.astype(bf16)
        kvb[r, b, w:, :] = jnp.dot(xb, wv_ref[...], preferred_element_type=f32).astype(bf16)
        q = jnp.dot(xb, wq_ref[...], preferred_element_type=f32)
        for h in range(heads):
            q_s[at, h * HEAD:(h + ONE) * HEAD] = turned(q[:, h * HEAD:(h + ONE) * HEAD]).astype(bf16)
        ycopy(dx, s, 0).start()
        ycopy(dx, s, ONE).start()

    def pass_on(dx, s):
        for k in (0, ONE):
            ycopy(dx, s, k, True).wait_recv()
        for k in (TWO, 3):
            ycopy(dx, s, k).start()

    xcopy(0).start()
    xcopy(ONE).start()
    sib(0).start()
    m_s[...] = jnp.full_like(m_s, -1e30)
    l_s[...] = jnp.zeros_like(l_s)
    acc_s[...] = jnp.zeros_like(acc_s)
    qkv(0, 0)
    sib(0, True).wait_recv()
    qkv(0, ONE)
    xcopy(0, True).wait_recv()
    xcopy(TWO).start()
    sib(nx - ONE).start()
    xcopy(ONE, True).wait_recv()
    xcopy(3).start()
    sib(ONE).start()
    qkv(nx - ONE, 0)
    qkv(ONE, 0)
    for dx in (nx - ONE, ONE):
        sib(dx, True).wait_recv()
        qkv(dx, ONE)
    for s in (0, ONE):
        pass_on(0, s)
    wstart(0)
    wstart(ONE)
    xcopy(TWO, True).wait_recv()
    xcopy(3, True).wait_recv()
    sib(TWO).start()
    qkv(TWO, 0)
    sib(TWO, True).wait_recv()
    qkv(TWO, ONE)

    def attend(h, qb, rank, kb, chunks, diag):
        rows = pl.ds(pl.multiple_of(qb * ntok, ntok), ntok)
        cols = slice(h * HEAD, (h + ONE) * HEAD)
        q = q_s[rows, cols]
        sc = []
        for j in range(chunks):
            t = jnp.dot(q, kvb[rank, kb + j, cols, :], preferred_element_type=f32)
            if diag and j == chunks - ONE:
                t = jnp.where(lax.broadcasted_iota(jnp.int32, t.shape, ONE) <= lax.broadcasted_iota(jnp.int32, t.shape, 0), t, -1e30)
            sc.append(t)
        m_old = m_s[h, rows, :]
        top = sc[0]
        for t in sc[ONE:]:
            top = jnp.maximum(top, t)
        m_new = jnp.maximum(m_old, jnp.max(top, axis=ONE, keepdims=True))
        alpha = jnp.exp2((m_old - m_new) * cexp)
        ps = [jnp.exp2((t - m_new[:, :ONE]) * cexp) for t in sc]
        tot = ps[0]
        for p in ps[ONE:]:
            tot = tot + p
        pv = None
        for j, p in enumerate(ps):
            t = jnp.dot(p.astype(bf16), kvb[rank, kb + j, w:, cols], preferred_element_type=f32)
            pv = t if pv is None else pv + t
        l_s[h, rows, :] = alpha * l_s[h, rows, :] + jnp.sum(tot, axis=ONE, keepdims=True)
        acc_s[h, rows, :] = alpha * acc_s[h, rows, :] + pv
        m_s[h, rows, :] = m_new

    per = nch // TWO

    def full(rank, qbase, kb):
        def go(i, _):
            for h in range(heads):
                attend(h, qbase + i, rank, kb, per, False)
            return 0

        lax.fori_loop(0, per, go, 0)

    def own_diag(second, _):
        base = second * per
        for i in range(per):
            for h in range(heads):
                attend(h, base + i, r, base, i + ONE, True)
        return 0

    lax.fori_loop(0, TWO, own_diag, 0)
    for dx in (nx - ONE, ONE):
        for s in (0, ONE):
            pass_on(dx, s)
    full(r, per, 0)
    for s in (0, ONE):
        pass_on(TWO, s)
    wpass(0)

    def other(dy):
        rank = (r + dy) % ncp
        low = jnp.where(rank < r, 0, per)
        full(rank, per, 0)
        full(rank, low, low)

    other(ONE)
    wlast(0)
    other(ncp - ONE)
    wpass(ONE)
    for dx in range(nx):
        for s in (0, ONE):
            for k in (TWO, 3):
                ycopy(dx, s, k, True).wait_recv()
    other(TWO)
    wlast(ONE)
    for h in range(heads):
        o_ref[:, h * HEAD:(h + ONE) * HEAD] = (acc_s[h] / l_s[h]).astype(bf16)

    wend(0)
    wend(ONE)
    for k in range(4):
        xcopy(k).wait_send()
    for dx in range(nx):
        sib(dx).wait_send()
        for s in (0, ONE):
            for k in range(4):
                ycopy(dx, s, k).wait_send()


def attention(x, g, wq, wk, wv, cos, sin, wo, ws2, ncp, ntp):
    ntok, dm = x.shape
    w = wq.shape[ONE]
    heads = w // HEAD
    n = ntok * ntp
    vm = pl.BlockSpec(memory_space=pltpu.VMEM)
    any_ = pl.BlockSpec(memory_space=pl.ANY)
    dma = pltpu.SemaphoreType.DMA
    return pl.pallas_call(
        attn_kernel,
        in_specs=[vm] * 7 + [any_] * TWO,
        out_specs=[vm, any_, any_],
        out_shape=[jax.ShapeDtypeStruct((n, w), bf16), jax.ShapeDtypeStruct((ntp,) + wo.shape, bf16),
                   jax.ShapeDtypeStruct((ntp,) + ws2.shape, bf16)],
        scratch_shapes=[pltpu.VMEM((ntp, ntok, dm), bf16), pltpu.VMEM((n, w), bf16), pltpu.VMEM((ncp, ntp, TWO * w, ntok), bf16),
                        pltpu.VMEM((heads, n, HEAD), f32), pltpu.VMEM((heads, n, HEAD), f32), pltpu.VMEM((heads, n, HEAD), f32),
                        dma((4,)), dma((4,)), dma((ntp // TWO,)), dma((ntp // TWO,)), dma((4 * ntp,)), dma((4 * ntp,)),
                        dma((TWO, 4)), dma((TWO, 4)), dma((TWO, ntp // TWO)), dma((TWO, ntp // TWO)), dma((TWO,))],
        compiler_params=pltpu.CompilerParams(collective_id=ONE, has_side_effects=True, vmem_limit_bytes=60 * TWO**20),
        cost_estimate=pl.CostEstimate(flops=6 * n * dm * w + TWO * n * n * ncp * w, bytes_accessed=16 * n * dm, transcendentals=0),
    )(x, g.reshape(ONE, dm), wq, wk, wv, cos, sin, wo, ws2)


ORDER = [(0, 0), (ONE, 0), (3, 0), (0, ONE), (0, 3), (TWO, 0), (0, TWO), (ONE, ONE),
         (ONE, 3), (3, ONE), (3, 3), (TWO, ONE), (TWO, 3), (ONE, TWO), (3, TWO), (TWO, TWO)]
DIST = [0, ONE, TWO, ONE]


def packed(values):
    return [sum(v << (TWO * i) for i, v in enumerate(values[k:k + 8])) for k in (0, 8)]


DX, DY = packed([o[0] for o in ORDER]), packed([o[ONE] for o in ORDER])


def look(table, j):
    a, b = table
    return ((a + (j // 8) * (b - a)) >> (TWO * (j % 8))) & 3


def gather_copies(rows):
    h, q = rows // TWO, rows // 4
    out = []
    for flip in (False, True):
        base = h if flip else 0
        fw = (lambda a, b: (b, a)) if flip else (lambda a, b: (a, b))

        def add(rank, blk, lo, n, step):
            out.append((rank, fw(*blk), base + lo, n, fw(*step)))

        add(0, (0, 0), 0, h, (ONE, 0))
        add(0, (0, 0), 0, h, (3, 0))
        add(ONE, (3, 0), 0, q, (ONE, 0))
        add(ONE, (ONE, 0), q, q, (3, 0))
        for b in (3, ONE, 0, TWO):
            add(TWO, (b, 0), 0, h, (0, ONE))
            add(TWO, (b, 0), 0, h, (0, 3))
            add(3, (b, 3), 0, q, (0, ONE))
            add(3, (b, ONE), q, q, (0, 3))
    out.sort(key=lambda t: t[0])
    return [t[ONE:] for t in out]


def dist(b):
    return DIST[b[0]] + DIST[b[ONE]]


def moe_kernel(nx, ny, cap, groups, t_ref, idx_ref, code_ref, gate_ref, w1g_ref, w1u_ref, w2_ref,
               ws1_ref, ws2_ref, acc_ref, tg_ref, rz_ref, ru_ref, md_ref,
               vg, vu, vd, xin, act, zb, tb, zin, ia, mc_ref,
               wsem, tsem, zsem, lsem, ag_s, ag_r, dd_s, dd_r, rt_s, rt_r, ix_s, ix_r,
               us_s, us_r, ssem, l1_s, l1_r, l2_s, l2_r):
    ntok, dm = t_ref.shape
    ff = w1g_ref.shape[TWO]
    y = lax.axis_index("cp")
    tp = lax.axis_index("tp")
    x, c = tp // TWO, tp % TWO
    nchip = nx * ny
    per = nchip // groups
    homes = TWO * per

    def dev(dx, dy, core):
        return {"cp": (y + dy) % ny, "tp": ((x + dx) % nx) * TWO + core}

    def flat(dx, dy, core):
        return ((y + dy) % ny) * (TWO * nx) + ((x + dx) % nx) * TWO + core

    def weights(l):
        return [pltpu.make_async_copy(a.at[l, pl.ds(k * (a.shape[ONE] // 4), a.shape[ONE] // 4), :],
                                      b.at[l, pl.ds(k * (a.shape[ONE] // 4), a.shape[ONE] // 4), :], wsem.at[l, n, k])
                for n, (a, b) in enumerate(((w1g_ref, vg), (w1u_ref, vu), (w2_ref, vd))) for k in range(4)]

    own = pltpu.make_async_copy(t_ref, tg_ref.at[flat(0, 0, c)], lsem.at[0])

    ia[flat(0, 0, c)] = idx_ref[...]
    barrier = pltpu.get_barrier_semaphore()

    def greet(k, _):
        other = (y * TWO * nx + tp + k) % (TWO * nchip)
        pl.semaphore_signal(barrier, inc=ONE, device_id={"cp": other // (TWO * nx), "tp": other % (TWO * nx)}, device_id_type=MESH)
        return 0

    lax.fori_loop(ONE, TWO * nchip, greet, 0)
    pl.semaphore_wait(barrier, TWO * nchip - ONE)

    copies = gather_copies(ntok)

    def ici(k):
        blk, lo, n, step = copies[k]
        here = tg_ref.at[flat(blk[0], blk[ONE], c), pl.ds(lo, n), :]
        src = t_ref.at[pl.ds(lo, n), :] if blk == (0, 0) else here
        return pltpu.make_async_remote_copy(src_ref=src, dst_ref=here, send_sem=ag_s.at[k], recv_sem=ag_r.at[k],
                                            device_id=dev(step[0], step[ONE], c), device_id_type=MESH)

    def ici_in(k):
        blk, lo, n, step = copies[k]
        here = tg_ref.at[flat(blk[0] - step[0] + nx, blk[ONE] - step[ONE] + ny, c), pl.ds(lo, n), :]
        return pltpu.make_async_remote_copy(src_ref=here, dst_ref=here, send_sem=ag_s.at[k], recv_sem=ag_r.at[k],
                                            device_id=dev(nx - step[0], ny - step[ONE], c), device_id_type=MESH)

    def d2d(j, core):
        blk = ORDER[j]
        here = tg_ref.at[flat(blk[0], blk[ONE], core)]
        src = t_ref if (j == 0) else here
        return pltpu.make_async_remote_copy(src_ref=src, dst_ref=here, send_sem=dd_s.at[j], recv_sem=dd_r.at[j],
                                            device_id=dev(0, 0, ONE - c), device_id_type=MESH)

    def d2d_in(j):
        blk = ORDER[j]
        here = tg_ref.at[flat(blk[0], blk[ONE], ONE - c)]
        return pltpu.make_async_remote_copy(src_ref=here, dst_ref=here, send_sem=dd_s.at[j], recv_sem=dd_r.at[j],
                                            device_id=dev(0, 0, ONE - c), device_id_type=MESH)

    def round_(w):
        h = ntok // TWO
        if w == 0:
            for k, cp in enumerate(copies):
                if cp[0] == (0, 0):
                    ici(k).start()
            d2d(0, c).start()
            return
        left = {}
        into = [(k, ((cp[0][0] - cp[3][0]) % nx, (cp[0][ONE] - cp[3][ONE]) % ny), cp) for k, cp in enumerate(copies) if dist(cp[0]) == w - ONE]
        for k, blk, cp in into:
            part = (blk, cp[ONE] // h)
            left[part] = left.get(part, 0) + cp[TWO]
        done = {}
        for k, blk, cp in into:
            ici_in(k).wait_recv()
            part = (blk, cp[ONE] // h)
            left[part] -= cp[TWO]
            if left[part] == 0:
                for n, out in enumerate(copies):
                    if out[0] == blk and out[ONE] // h == part[ONE]:
                        ici(n).start()
                done[blk] = done.get(blk, 0) + ONE
                if done[blk] == TWO:
                    d2d(ORDER.index(blk), c).start()

    def siblings(w):
        for j, b in enumerate(ORDER):
            if dist(b) == w:
                d2d_in(j).wait_recv()

    def choices(j, s, incoming=False):
        core = c if s == 0 else ONE - c
        dx, dy = look(DX, j), look(DY, j)
        ref = ia.at[flat(nx - dx, ny - dy, core) if incoming else flat(0, 0, c)]
        return pltpu.make_async_remote_copy(src_ref=ref, dst_ref=ref, send_sem=ix_s.at[TWO * j + s], recv_sem=ix_r.at[TWO * j + s],
                                            device_id=dev(nx - dx, ny - dy, core) if incoming else dev(dx, dy, core),
                                            device_id_type=MESH)

    def each_other(do):
        def go(j, _):
            @pl.when(j > 0)
            def _():
                do(j, 0)

            do(j, ONE)
            return 0

        lax.fori_loop(0, nchip, go, 0)

    each_other(lambda j, s: choices(j, s).start())
    round_(0)
    own.start()
    for l in range(TWO):
        for p in weights(l):
            p.start()

    def back(j, s, slot):
        core = c if s == 0 else ONE - c
        return pltpu.make_async_remote_copy(src_ref=zb.at[slot], dst_ref=rz_ref.at[slot], send_sem=rt_s.at[slot],
                                            recv_sem=rt_r.at[slot],
                                            device_id=dev(look(DX, j), look(DY, j), core), device_id_type=MESH)

    straight = sum(0 in o for o in ORDER)

    def cols(half):
        return pl.ds(half * (dm // TWO), dm // TWO)

    def leg1(j, half, incoming=False):
        dx, dy = ORDER[j]
        step = (0, dy) if half else (dx, 0)
        if incoming:
            step = (nx - step[0], ny - step[ONE])
        return pltpu.make_async_remote_copy(src_ref=zb.at[pl.ds(TWO * j, TWO), :, cols(half)], dst_ref=md_ref.at[j - straight, half],
                                            send_sem=l1_s.at[j - straight, half], recv_sem=l1_r.at[j - straight, half],
                                            device_id=dev(step[0], step[ONE], c), device_id_type=MESH)

    def leg2(j, s, half):
        step = (look(DX, j), 0) if half else (0, look(DY, j))
        return pltpu.make_async_remote_copy(src_ref=md_ref.at[j - straight, half, s], dst_ref=rz_ref.at[TWO * j + s, :, cols(half)],
                                            send_sem=l2_s.at[j - straight, s, half], recv_sem=l2_r.at[j - straight, s, half],
                                            device_id=dev(step[0], step[ONE], ONE - c if s else c), device_id_type=MESH)

    def leg2_in(j, s, half):
        step = (look(DX, j), 0) if half else (0, look(DY, j))
        return pltpu.make_async_remote_copy(src_ref=md_ref.at[j - straight, half, s], dst_ref=rz_ref.at[TWO * j + s, :, cols(half)],
                                            send_sem=l2_s.at[j - straight, s, half], recv_sem=l2_r.at[j - straight, s, half],
                                            device_id=dev(nx - step[0], ny - step[ONE], ONE - c if s else c), device_id_type=MESH)

    def forward(j):
        for half in range(TWO):
            leg1(j, half, True).wait_recv()
            for s in range(TWO):
                leg2(j, s, half).start()

    wide = ws1_ref.shape[ONE] // TWO
    deep = ws2_ref.shape[ONE]

    def ublock(i):
        return xin.at[i // nx, pl.ds(0, ntok), pl.ds((i % nx) * wide, wide)]

    def ucopy(i, incoming=False):
        dx, core = i // TWO, c if i % TWO == 0 else ONE - c
        return pltpu.make_async_remote_copy(src_ref=ublock(i), dst_ref=ru_ref.at[i], send_sem=us_s.at[i], recv_sem=us_r.at[i],
                                            device_id=dev(nx - dx if incoming else dx, 0, core), device_id_type=MESH)

    def uown():
        return pltpu.make_async_copy(ublock(0), ru_ref.at[0], us_s.at[0])

    def ws2_load(i):
        j = ((x + nx - i // TWO) % nx) * TWO + (c if i % TWO == 0 else ONE - c)
        return pltpu.make_async_copy(ws2_ref.at[j], vd.at[i // nx, pl.ds((i % nx) * deep, deep), :], ssem.at[ONE + i])

    def shared_up():
        first = pltpu.make_async_copy(ws1_ref, vg.at[0, :, pl.ds(0, TWO * wide)], ssem.at[0])
        first.start()

        def rows_of(i):
            d = flat(i // TWO, 0, c if i % TWO == 0 else ONE - c)
            return pltpu.make_async_copy(tg_ref.at[d], tb.at[i % DEPTH], tsem.at[i % DEPTH])

        for i in range(DEPTH - ONE):
            rows_of(i).start()
        for i in range(TWO * nx):
            ws2_load(i).start()
        first.wait()
        for i in range(TWO * nx):
            rows_of(i).wait()
            if i + DEPTH - ONE < TWO * nx:
                rows_of(i + DEPTH - ONE).start()
            a = jnp.dot(tb[i % DEPTH], vg[0, :, :wide], preferred_element_type=f32)
            b = jnp.dot(tb[i % DEPTH], vg[0, :, wide:TWO * wide], preferred_element_type=f32)
            xin[i // nx, :ntok, (i % nx) * wide:(i % nx + ONE) * wide] = (a * jax.nn.sigmoid(a) * b).astype(bf16)
        uown().start()
        for i in range(ONE, TWO * nx):
            ucopy(i).start()

    def shared_down():
        uown().wait()
        pulls = []
        for i in range(TWO * nx):
            if i:
                ucopy(i, True).wait_recv()
            p = pltpu.make_async_copy(ru_ref.at[i], tb.at[i // nx, :, pl.ds((i % nx) * wide, wide)], ssem.at[9 + i])
            p.start()
            pulls.append(p)
        for i in range(TWO * nx):
            ws2_load(i).wait()
            pulls[i].wait()

        def col(n, _):
            at = pl.ds(pl.multiple_of(n * 256, 256), 256)
            tot = acc_ref[:, at]
            for i in range(TWO * nx):
                tot = tot + jnp.dot(tb[i // nx, :, (i % nx) * wide:(i % nx) * wide + deep],
                                    vd[i // nx, (i % nx) * deep:(i % nx + ONE) * deep, at], preferred_element_type=f32)
            acc_ref[:, at] = tot
            return 0

        lax.fori_loop(0, dm // 256, col, 0)

    def work(g, _):
        for w in range(ONE, 5):
            @pl.when(g == w - ONE)
            def _():
                round_(w)
                if w == ONE:
                    siblings(0)
                siblings(w)
                if w == ONE:
                    own.wait()
                    each_other(lambda j, s: choices(j, s, True).wait_recv())
                    upto = (lax.broadcasted_iota(jnp.int32, (ntok, ntok), 0)
                            <= lax.broadcasted_iota(jnp.int32, (ntok, ntok), ONE)).astype(f32).astype(bf16)
                    for l in range(TWO):
                        e = (y * TWO * nx + tp) * TWO + l
                        hit = jnp.zeros((TWO * nchip, ntok), jnp.bool_)
                        for k in range(code_ref.shape[ONE]):
                            hit = hit | (ia[:, k, :] == e)
                        hit = hit.astype(f32)
                        cum = jnp.dot(hit.astype(bf16), upto, preferred_element_type=f32)
                        mc_ref[l] = (hit * cum).astype(jnp.int32)

        @pl.when(g == groups - ONE)
        def _():
            forward(straight)

        def fetch(i):
            j = g * per + i // TWO
            core = c if i % TWO == 0 else ONE - c
            d = flat(look(DX, j), look(DY, j), core)
            return d, pltpu.make_async_copy(tg_ref.at[d], tb.at[i % DEPTH], tsem.at[i % DEPTH])

        for i in range(DEPTH - ONE):
            fetch(i)[ONE].start()
        for i in range(homes):
            d, cp = fetch(i)
            cp.wait()
            if i + DEPTH - ONE < homes:
                fetch(i + DEPTH - ONE)[ONE].start()
            rows = lax.broadcasted_iota(jnp.int32, (TWO * cap, ntok), 0)
            rank = jnp.where(rows < cap, mc_ref[0, pl.ds(d, ONE), :], mc_ref[ONE, pl.ds(d, ONE), :])
            sel = (rank == jnp.where(rows < cap, rows, rows - cap) + ONE).astype(f32).astype(bf16)
            for n in range(0, dm, 512):
                got = jnp.dot(sel, tb[i % DEPTH, :, n:n + 512], preferred_element_type=f32)
                xin[0, i * cap:(i + ONE) * cap, n:n + 512] = got[:cap].astype(bf16)
                xin[ONE, i * cap:(i + ONE) * cap, n:n + 512] = got[cap:].astype(bf16)

        for l in range(TWO):
            @pl.when(g == 0)
            def _():
                for p in weights(l):
                    p.wait()

            def up(at, n):
                a = jnp.dot(xin[l], vg[l, :, pl.ds(at, n)], preferred_element_type=f32)
                b = jnp.dot(xin[l], vu[l, :, pl.ds(at, n)], preferred_element_type=f32)
                act[:, pl.ds(at, n)] = (a * jax.nn.sigmoid(a) * b).astype(bf16)

            whole = ff // 256
            lax.fori_loop(0, whole, lambda n, _: (up(pl.multiple_of(n * 256, 256), 256), 0)[ONE], 0)
            if ff % 256:
                up(whole * 256, ff % 256)

            def down(n, _):
                at = pl.multiple_of(n * 256, 256)
                z = jnp.dot(act[...], vd[l, :, pl.ds(at, 256)], preferred_element_type=f32)
                for i in range(homes):
                    zb[g * homes + i, l * cap:(l + ONE) * cap, pl.ds(at, 256)] = z[i * cap:(i + ONE) * cap].astype(bf16)
                return 0

            lax.fori_loop(0, dm // 256, down, 0)

        @pl.when(g == 0)
        def _():
            pltpu.make_async_copy(zb.at[0], rz_ref.at[0], lsem.at[ONE]).start()

        for k in range(groups):
            @pl.when(g == k)
            def _():
                if k == groups - ONE:
                    shared_up()
                mine = range(k * per, (k + ONE) * per)
                for j in mine:
                    if j >= straight:
                        leg1(j, 0).start()
                        leg1(j, ONE).start()
                for s in range(TWO):
                    for j in mine:
                        if j < straight and j + s:
                            back(j, s, TWO * j + s).start()

        return 0

    lax.fori_loop(0, groups, work, 0)
    for j in range(straight + ONE, nchip):
        forward(j)

    acc_ref[...] = jnp.zeros_like(acc_ref)

    def arrived(j, s, slot):
        core = c if s == 0 else ONE - c
        return pltpu.make_async_remote_copy(src_ref=zb.at[slot], dst_ref=rz_ref.at[slot], send_sem=rt_s.at[slot],
                                            recv_sem=rt_r.at[slot],
                                            device_id=dev(nx - look(DX, j), ny - look(DY, j), core), device_id_type=MESH)

    def combine(j, _):
        @pl.when(j == nchip - per)
        def _():
            shared_down()

        @pl.when(j == 0)
        def _():
            pltpu.make_async_copy(zb.at[0], rz_ref.at[0], lsem.at[ONE]).wait()

        @pl.when((j > 0) & (j < straight))
        def _():
            arrived(j, 0, TWO * j).wait_recv()

        @pl.when(j < straight)
        def _():
            arrived(j, ONE, TWO * j + ONE).wait_recv()

        @pl.when(j >= straight)
        def _():
            for s in range(TWO):
                for half in range(TWO):
                    leg2_in(j, s, half).wait_recv()

        pulls = [pltpu.make_async_copy(rz_ref.at[TWO * j + s], zin.at[pl.ds(s * TWO * cap, TWO * cap), :], zsem.at[s]) for s in range(TWO)]
        for p in pulls:
            p.start()
        base = [flat(nx - look(DX, j), ny - look(DY, j), core) * (TWO * cap) for core in (c, ONE - c)]
        lane = lax.broadcasted_iota(jnp.int32, (ntok, 4 * cap), ONE)
        want = jnp.where(lane < TWO * cap, base[0] + lane, base[ONE] + lane - TWO * cap)
        g = jnp.zeros((ntok, 4 * cap), f32)
        for k in range(code_ref.shape[ONE]):
            g = g + jnp.where(code_ref[:, k:k + ONE] == want, gate_ref[:, k:k + ONE], 0.0)
        g1 = g.astype(bf16)
        rest = g - g1.astype(f32)
        g2 = rest.astype(bf16)
        g3 = (rest - g2.astype(f32)).astype(bf16)
        for p in pulls:
            p.wait()

        def col(n, _):
            at = pl.ds(pl.multiple_of(n * 512, 512), 512)
            z = zin[:, at]
            acc_ref[:, at] += (jnp.dot(g1, z, preferred_element_type=f32)
                               + (jnp.dot(g2, z, preferred_element_type=f32) + jnp.dot(g3, z, preferred_element_type=f32)))
            return 0

        lax.fori_loop(0, dm // 512, col, 0)
        return 0

    lax.fori_loop(0, nchip, combine, 0)

    for k in range(len(copies)):
        ici(k).wait_send()
    for j in range(nchip):
        d2d(j, c).wait_send()

    each_other(lambda j, s: choices(j, s).wait_send())
    for j in range(nchip):
        for s in range(TWO):
            if j >= straight:
                leg1(j, s).wait_send()
                for half in range(TWO):
                    leg2(j, s, half).wait_send()
            elif j + s:
                back(j, s, TWO * j + s).wait_send()
    for i in range(ONE, TWO * nx):
        ucopy(i).wait_send()


def moe(t, idx, code, gates, w1g, w1u, w2, ws1, ws2, nx, ny, cap):
    ntok, dm = t.shape
    nle, _, ff = w1g.shape
    ndev = TWO * nx * ny
    groups = 4
    rows = ndev // groups * cap
    any_ = pl.BlockSpec(memory_space=pl.ANY)
    vm = pl.BlockSpec(memory_space=pltpu.VMEM)
    ncopy = len(gather_copies(ntok))
    turns = sum(0 not in o for o in ORDER)
    dma = pltpu.SemaphoreType.DMA
    return pl.pallas_call(
        functools.partial(moe_kernel, nx, ny, cap, groups),
        in_specs=[vm, vm, vm, vm] + [any_] * 5,
        out_specs=[vm] + [any_] * 4,
        out_shape=[jax.ShapeDtypeStruct((ntok, dm), f32),
                   jax.ShapeDtypeStruct((ndev, ntok, dm), bf16),
                   jax.ShapeDtypeStruct((ndev, nle * cap, dm), bf16),
                   jax.ShapeDtypeStruct((TWO * nx, ntok, ws1.shape[ONE] // TWO), bf16),
                   jax.ShapeDtypeStruct((turns, TWO, TWO, nle * cap, dm // TWO), bf16)],
        scratch_shapes=[pltpu.VMEM((nle, dm, ff), bf16), pltpu.VMEM((nle, dm, ff), bf16), pltpu.VMEM((nle, ff, dm), bf16),
                        pltpu.VMEM((nle, rows, dm), bf16), pltpu.VMEM((rows, ff), bf16),
                        pltpu.VMEM((ndev, nle * cap, dm), bf16), pltpu.VMEM((DEPTH, ntok, dm), bf16),
                        pltpu.VMEM((TWO * nle * cap, dm), bf16), pltpu.VMEM((ndev,) + idx.shape, jnp.int32),
                        pltpu.VMEM((nle, ndev, ntok), jnp.int32),
                        dma((TWO, 3, 4)), dma((DEPTH,)), dma((TWO,)), dma((TWO,)), dma((ncopy,)), dma((ncopy,)),
                        dma((nx * ny,)), dma((nx * ny,)), dma((ndev,)), dma((ndev,)), dma((ndev,)), dma((ndev,)),
                        dma((TWO * nx,)), dma((TWO * nx,)), dma((17,)), dma((turns, TWO)), dma((turns, TWO)),
                        dma((turns, TWO, TWO)), dma((turns, TWO, TWO))],
        compiler_params=pltpu.CompilerParams(collective_id=0, has_side_effects=True, vmem_limit_bytes=VMEM_MAX),
        cost_estimate=pl.CostEstimate(flops=6 * ndev * nle * cap * dm * ff, bytes_accessed=10 * nle * dm * ff, transcendentals=0),
    )(t, idx, code, gates, w1g, w1u, w2, ws1, ws2)


def solution(mesh):
    ncp = mesh.shape["cp"]
    ntp = mesh.shape["tp"]
    ndev = ncp * ntp
    rows = P(("dp", "cp", "tp"), None)
    cols = P(None, "tp")
    wrows = P("tp", None)
    rep = P(None)
    exps = P(("cp", "tp"), None, None)

    def layer(x, g_attn, wq, wk, wv, wo, g_mlp, idx, gates, w1g, w1u, w2, ws1g, ws1u, ws2):
        r = lax.axis_index("cp")
        me = r * ntp + lax.axis_index("tp")
        ntok, dm = x.shape
        seq = ntok * ndev
        nloc = seq // ncp
        nle = w1g.shape[0]
        num_e = nle * ndev
        top = idx.shape[ONE]
        cap = -(-top * (TWO * ntok // num_e + ONE) // 8) * 8

        upto = (jnp.arange(ntok)[:, None] <= jnp.arange(ntok)[None, :]).astype(bf16)
        named = idx[:, :, None] == jnp.arange(num_e)[None, None, :]
        before = lax.dot_general(upto, jnp.any(named, axis=ONE).astype(bf16), (((0,), (0,)), ((), ())), preferred_element_type=f32) - 1.0
        rank = jnp.sum(jnp.where(named, before[:, None, :], 0.0), axis=-ONE).astype(jnp.int32)
        code = idx * cap + rank

        half = HEAD // TWO
        pos = layout_pos(r * nloc + jnp.arange(nloc), ncp, seq)
        freq = ROPE_BASE ** (-jnp.arange(half, dtype=f32) / half)
        ang = pos.astype(f32)[:, None] * freq[None, :]
        cs, sn = jnp.cos(ang), jnp.sin(ang)
        o, wo_all, ws2_all = attention(x, g_attn, wq, wk, wv, jnp.concatenate([cs, cs], ONE), jnp.concatenate([-sn, sn], ONE), wo, ws2, ncp, ntp)
        o = lax.all_to_all(o, "tp", 0, ONE, tiled=True)
        attn = jnp.dot(o, wo_all.reshape(-ONE, dm), preferred_element_type=f32)
        h = (x.astype(f32) + attn).astype(bf16)
        t = rms_norm(h, g_mlp)

        idx_t = jnp.pad(idx.T, ((0, 8 - top), (0, 0)), constant_values=-ONE)
        pad = ((0, 0), (0, -ws1g.shape[ONE] % 128))
        ws1 = jnp.concatenate([jnp.pad(ws1g, pad), jnp.pad(ws1u, pad)], axis=ONE)
        added = moe(t, idx_t, code, gates, w1g, w1u, w2, ws1, ws2_all, ntp // TWO, ncp, cap)[0]
        return (h.astype(f32) + added).astype(bf16)

    return jax.shard_map(layer, mesh=mesh,
                         in_specs=(rows, rep, cols, cols, cols, wrows, rep, rows, rows, exps, exps, exps, cols, cols, wrows),
                         out_specs=rows, check_vma=False)
```

time: 544 us -> 503 us (0.925)
  the two profiles are of different devices: /device:TPU:97 before, /device:TPU:98 now
where the time goes in v3:
time: 503 us; the launch traced here: 493 us
  Pallas kernels  454 us (90%)
  other arithmetic  12.1 us (2%)
  waiting for transfers between devices  7.52 us (1%)
  starting transfers between devices  6.83 us (1%)
  matrix products  6.56 us (1%)
  local copies, waits for them, and re-layouts  5.95 us (1%)
    pallas_call x1, Pallas kernels, moe(): pl.pallas_call(functools.partial(moe_kernel, nx, ny, cap, groups), in_spe...  313 us
    pallas_call x1, Pallas kernels, attention(): pl.pallas_call(attn_kernel, in_specs=[vm] * 7 + [any_] * TWO, out_specs=[...  142 us
  transfers between devices with their start and end apart: 1, of which 1 were waited for; matrix products, arithmetic and copies ran while one was open for 1% of the time, Pallas kernels for 0%

profile of v3, /device:TPU:98, one launch (start us, length us, event | category | flops | bytes accessed | tf_op | source)
XLA Modules:
  0.0 493.4 jit_solution(7633713329975436644)
XLA Ops:
  0.0 3.7 fusion.11
  3.8 2.0 pad_maximum_fusion
  5.8 0.0 copy-start.2
  5.8 141.5 %shard_map.145 = (bf16[2048,256]{1,0:T(8,128)(2,1)}, bf16[8,256,2048]{2,1,0:T(8,128)(2,1)}, bf16[8,352,2048]{2,1,0:T(8,128)(2,1)}) custom-call(bf16[256,2048]{1,0:T(8,128)(2,1)} %x_ref.1, f32[1,2048]{1,0:T(1,128)} %bitcast.18, bf16[2048,256]{1,0:T(8,128)(2,1)} %wq_ref.1, bf16[2048,256]{1,0:T(8,128)(2,1)} %wk_ref.1, bf16[2048,256]{1,0:T(8,128)(2,1)} %wv_ref.1, ...), custom_call_target="tpu_custom_call" | custom-call | flops 15032385536 | bytes 67108864 | tf_op jit(solution)/shard_map/pallas_call | solution.py:293
  147.3 0.0 copy-start.1
  147.3 6.8 %all-to-all-start = ((bf16[8,256,256]{2,1,0:T(8,128)(2,1)}), bf16[8,256,256]{2,1,0:T(8,128)(2,1)}, u32[]{:S(2)}, u32[]{:S(2)}) async-start(bf16[8,256,256]{2,1,0:T(8,128)(2,1)} %bitcast.16), calls=%async_computation | async-start | bytes 2097152 | tf_op jit(solution)/shard_map/all_to_all | solution.py:820
  154.1 0.0 copy-done.2
  154.2 0.2 convolution_add_fusion
  154.3 0.1 select_reduce_fusion
  154.4 0.8 copy.31.code_ref
  155.2 0.0 copy-done.4
  155.2 0.8 copy.32.gate_ref
  156.0 0.0 copy-done.1
  156.0 0.8 copy.29
  156.9 1.9 copy.30
  158.7 0.6 pad.11.idx_ref
  159.3 1.9 fusion.2.ws1_ref
  161.2 7.5 %all-to-all-done = bf16[8,256,256]{2,1,0:T(8,128)(2,1)} async-done(((bf16[8,256,256]{2,1,0:T(8,128)(2,1)}), bf16[8,256,256]{2,1,0:T(8,128)(2,1)}, u32[]{:S(2)}, u32[]{:S(2)}) %all-to-all-start) | async-done | bytes 1048608 | tf_op jit(solution)/shard_map/all_to_all | solution.py:820
  168.7 6.4 %fusion.5 = (f32[256]{0:T(256)S(1)}, bf16[256,2048]{1,0:T(8,128)(2,1)S(1)}) fusion(bf16[8,256,2048]{2,1,0:T(8,128)(2,1)} %get-tuple-element.10, bf16[8,256,256]{2,1,0:T(8,128)(2,1)} %all-to-all-done, bf16[256,2048]{1,0:T(8,128)(2,1)} %x_ref.1), kind=kOutput, calls=%fused_computation.11 | convolution fusion | flops 2150629120 | bytes 11535360 | tf_op jit(solution)/shard_map/dot_general | solution.py:821
  175.2 1.0 copy-done
  176.2 0.0 copy-done.3
  176.2 1.3 fusion.7.t_ref
  177.5 312.6 %shard_map.146 = (f32[256,2048]{1,0:T(8,128)}, bf16[32,256,2048]{2,1,0:T(8,128)(2,1)}, bf16[32,112,2048]{2,1,0:T(8,128)(2,1)}, bf16[8,256,384]{2,1,0:T(8,128)(2,1)}, bf16[9,2,2,112,1024]{4,3,2,1,0:T(8,128)(2,1)}) custom-call(bf16[256,2048]{1,0:T(8,128)(2,1)} %fusion.7.t_ref, s32[8,256]{1,0:T(8,128)} %pad.11.idx_ref, s32[256,6]{1,0:T(8,128)} %copy.31.code_ref, ...), custom_call_target="tpu_custom_call" | custom-call | flops 62008590336 | bytes 57671680 | tf_op jit(solution)/shard_map/pallas_call | solution.py:764
  490.1 3.1 fusion.8
  (8 shorter events, 0.1 us)
Async XLA Ops:
  5.8 148.4 %copy-start.2 = (s32[256,6]{0,1:T(8,128)S(1)}, s32[256,6]{0,1:T(8,128)}, u32[]{:S(2)}) copy-start(s32[256,6]{0,1:T(8,128)} %param.22) | copy-start | bytes 18436
  5.8 149.5 %copy-start.4 = (f32[256,6]{0,1:T(8,128)S(1)}, f32[256,6]{0,1:T(8,128)}, u32[]{:S(2)}) copy-start(f32[256,6]{0,1:T(8,128)} %param.23) | copy-start | bytes 18436
  147.3 8.7 %copy-start.1 = (bf16[2048,352]{0,1:T(8,128)(2,1)S(1)}, bf16[2048,352]{0,1:T(8,128)(2,1)}, u32[]{:S(2)}) copy-start(bf16[2048,352]{0,1:T(8,128)(2,1)} %param.27) | copy-start | bytes 4325380
  147.3 21.4 %all-to-all-start = ((bf16[8,256,256]{2,1,0:T(8,128)(2,1)}), bf16[8,256,256]{2,1,0:T(8,128)(2,1)}, u32[]{:S(2)}, u32[]{:S(2)}) async-start(bf16[8,256,256]{2,1,0:T(8,128)(2,1)} %bitcast.16), calls=%async_computation | async-start | bytes 2097152 | tf_op jit(solution)/shard_map/all_to_all | solution.py:820
  168.7 7.5 %copy-start.3 = (f32[2048]{0:T(1024)S(1)}, f32[2048]{0:T(1024)}, u32[]{:S(2)}) copy-start(f32[2048]{0:T(1024)} %param.21) | copy-start | bytes 24580
  175.1 1.1 copy-start

commit v4 on v3

--- a/solution.py
+++ b/solution.py
@@ -85,7 +85,7 @@
         rows = kvb.shape[TWO]
         lo, num = ((0, rows), (0, rows), (0, rows // TWO), (rows // TWO, rows // TWO))[k]
         at = (src - step) % ncp if incoming else src
-        b = block(dx, c if s == 0 else ONE - c)
+        b = block(dx, (c + s) % TWO)
         ref = kvb.at[(r + at) % ncp, b, pl.ds(lo, num), :]
         sem = (dx * TWO + s) * 4 + k
         return pltpu.make_async_remote_copy(src_ref=ref, dst_ref=ref, send_sem=ys.at[sem], recv_sem=yr.at[sem],
@@ -143,7 +143,7 @@
             wsib(a, dx).wait_send()
 
     def qkv(dx, s):
-        b = block(dx, c if s == 0 else ONE - c)
+        b = block(dx, (c + s) % TWO)
         at = pl.ds(pl.multiple_of(b * ntok, ntok), ntok)
         xb = xg[b]
         cs, sn = c_ref[at, :], s_ref[at, :]
@@ -173,30 +173,43 @@
     m_s[...] = jnp.full_like(m_s, -1e30)
     l_s[...] = jnp.zeros_like(l_s)
     acc_s[...] = jnp.zeros_like(acc_s)
-    qkv(0, 0)
-    sib(0, True).wait_recv()
-    qkv(0, ONE)
-    xcopy(0, True).wait_recv()
-    xcopy(TWO).start()
-    sib(nx - ONE).start()
-    xcopy(ONE, True).wait_recv()
-    xcopy(3).start()
-    sib(ONE).start()
-    qkv(nx - ONE, 0)
-    qkv(ONE, 0)
-    for dx in (nx - ONE, ONE):
-        sib(dx, True).wait_recv()
-        qkv(dx, ONE)
-    for s in (0, ONE):
-        pass_on(0, s)
-    wstart(0)
-    wstart(ONE)
-    xcopy(TWO, True).wait_recv()
-    xcopy(3, True).wait_recv()
-    sib(TWO).start()
-    qkv(TWO, 0)
-    sib(TWO, True).wait_recv()
-    qkv(TWO, ONE)
+    order = ((0, 0), (0, ONE), (nx - ONE, 0), (ONE, 0), (nx - ONE, ONE), (ONE, ONE), (TWO, 0), (TWO, ONE))
+    dxs = sum(o[0] << (TWO * i) for i, o in enumerate(order))
+    other = sum(o[ONE] << i for i, o in enumerate(order))
+
+    def chunk(n, _):
+        @pl.when(n == ONE)
+        def _():
+            sib(0, True).wait_recv()
+
+        @pl.when(n == TWO)
+        def _():
+            xcopy(0, True).wait_recv()
+            xcopy(TWO).start()
+            sib(nx - ONE).start()
+            xcopy(ONE, True).wait_recv()
+            xcopy(TWO + ONE).start()
+            sib(ONE).start()
+            wstart(0)
+            wstart(ONE)
+
+        for i, dx in ((4, nx - ONE), (5, ONE), (7, TWO)):
+            @pl.when(n == i)
+            def _():
+                sib(dx, True).wait_recv()
+
+        @pl.when(n == 6)
+        def _():
+            for s in (0, ONE):
+                pass_on(0, s)
+            xcopy(TWO, True).wait_recv()
+            xcopy(TWO + ONE, True).wait_recv()
+            sib(TWO).start()
+
+        qkv((dxs >> (TWO * n)) & 3, (other >> n) & ONE)
+        return 0
+
+    lax.fori_loop(0, nch, chunk, 0)
 
     def attend(h, qb, rank, kb, chunks, diag):
         rows = pl.ds(pl.multiple_of(qb * ntok, ntok), ntok)
@@ -214,7 +227,8 @@
             top = jnp.maximum(top, t)
         m_new = jnp.maximum(m_old, jnp.max(top, axis=ONE, keepdims=True))
         alpha = jnp.exp2((m_old - m_new) * cexp)
-        ps = [jnp.exp2((t - m_new[:, :ONE]) * cexp) for t in sc]
+        level = jnp.concatenate([m_new] * (ntok // HEAD), axis=ONE)
+        ps = [jnp.exp2((t - level) * cexp) for t in sc]
         tot = ps[0]
         for p in ps[ONE:]:
             tot = tot + p
@@ -222,19 +236,11 @@
         for j, p in enumerate(ps):
             t = jnp.dot(p.astype(bf16), kvb[rank, kb + j, w:, cols], preferred_element_type=f32)
             pv = t if pv is None else pv + t
-        l_s[h, rows, :] = alpha * l_s[h, rows, :] + jnp.sum(tot, axis=ONE, keepdims=True)
+        l_s[h, rows, :] = alpha * l_s[h, rows, :] + sum(tot[:, n:n + HEAD] for n in range(0, ntok, HEAD))
         acc_s[h, rows, :] = alpha * acc_s[h, rows, :] + pv
         m_s[h, rows, :] = m_new
 
     per = nch // TWO
-
-    def full(rank, qbase, kb):
-        def go(i, _):
-            for h in range(heads):
-                attend(h, qbase + i, rank, kb, per, False)
-            return 0
-
-        lax.fori_loop(0, per, go, 0)
 
     def own_diag(second, _):
         base = second * per
@@ -244,32 +250,48 @@
         return 0
 
     lax.fori_loop(0, TWO, own_diag, 0)
-    for dx in (nx - ONE, ONE):
-        for s in (0, ONE):
-            pass_on(dx, s)
-    full(r, per, 0)
-    for s in (0, ONE):
-        pass_on(TWO, s)
-    wpass(0)
-
-    def other(dy):
+    def ranks(k, _):
+        @pl.when(k == 0)
+        def _():
+            for dx in (nx - ONE, ONE):
+                for s in (0, ONE):
+                    pass_on(dx, s)
+
+        @pl.when(k == ONE)
+        def _():
+            for s in (0, ONE):
+                pass_on(TWO, s)
+            wpass(0)
+
+        @pl.when(k == TWO)
+        def _():
+            wlast(0)
+
+        @pl.when(k == ncp - ONE)
+        def _():
+            wpass(ONE)
+            for dx in range(nx):
+                for s in (0, ONE):
+                    for n in (TWO, TWO + ONE):
+                        ycopy(dx, s, n, True).wait_recv()
+
+        dy = jnp.where(k == TWO, ncp - ONE, jnp.where(k == ncp - ONE, TWO, k))
         rank = (r + dy) % ncp
         low = jnp.where(rank < r, 0, per)
-        full(rank, per, 0)
-        full(rank, low, low)
-
-    other(ONE)
-    wlast(0)
-    other(ncp - ONE)
-    wpass(ONE)
-    for dx in range(nx):
-        for s in (0, ONE):
-            for k in (TWO, 3):
-                ycopy(dx, s, k, True).wait_recv()
-    other(TWO)
+
+        def go(i, _):
+            turn = i // per
+            for h in range(heads):
+                attend(h, jnp.where(turn == 0, per, low) + i % per, rank, turn * low, per, False)
+            return 0
+
+        lax.fori_loop(0, jnp.where(k == 0, per, TWO * per), go, 0)
+        return 0
+
+    lax.fori_loop(0, ncp, ranks, 0)
     wlast(ONE)
     for h in range(heads):
-        o_ref[:, h * HEAD:(h + ONE) * HEAD] = (acc_s[h] / l_s[h]).astype(bf16)
+        o_ref[:, h * HEAD:(h + ONE) * HEAD] = (acc_s[h] / jnp.sum(l_s[h], axis=ONE, keepdims=True)).astype(bf16)
 
     wend(0)
     wend(ONE)
@@ -292,7 +314,7 @@
     dma = pltpu.SemaphoreType.DMA
     return pl.pallas_call(
         attn_kernel,
-        in_specs=[vm] * 7 + [any_] * TWO,
+        in_specs=[vm] * 9,
         out_specs=[vm, any_, any_],
         out_shape=[jax.ShapeDtypeStruct((n, w), bf16), jax.ShapeDtypeStruct((ntp,) + wo.shape, bf16),
                    jax.ShapeDtypeStruct((ntp,) + ws2.shape, bf16)],
@@ -618,12 +640,16 @@
             rows = lax.broadcasted_iota(jnp.int32, (TWO * cap, ntok), 0)
             rank = jnp.where(rows < cap, mc_ref[0, pl.ds(d, ONE), :], mc_ref[ONE, pl.ds(d, ONE), :])
             sel = (rank == jnp.where(rows < cap, rows, rows - cap) + ONE).astype(f32).astype(bf16)
-            for n in range(0, dm, 512):
-                got = jnp.dot(sel, tb[i % DEPTH, :, n:n + 512], preferred_element_type=f32)
-                xin[0, i * cap:(i + ONE) * cap, n:n + 512] = got[:cap].astype(bf16)
-                xin[ONE, i * cap:(i + ONE) * cap, n:n + 512] = got[cap:].astype(bf16)
-
-        for l in range(TWO):
+            def pick(n, _):
+                at = pl.ds(pl.multiple_of(n * 1024, 1024), 1024)
+                got = jnp.dot(sel, tb[i % DEPTH, :, at], preferred_element_type=f32)
+                xin[0, i * cap:(i + ONE) * cap, at] = got[:cap].astype(bf16)
+                xin[ONE, i * cap:(i + ONE) * cap, at] = got[cap:].astype(bf16)
+                return 0
+
+            lax.fori_loop(0, dm // 1024, pick, 0)
+
+        def expert(l, _):
             @pl.when(g == 0)
             def _():
                 for p in weights(l):
@@ -642,11 +668,17 @@
             def down(n, _):
                 at = pl.multiple_of(n * 256, 256)
                 z = jnp.dot(act[...], vd[l, :, pl.ds(at, 256)], preferred_element_type=f32)
-                for i in range(homes):
-                    zb[g * homes + i, l * cap:(l + ONE) * cap, pl.ds(at, 256)] = z[i * cap:(i + ONE) * cap].astype(bf16)
+                for k in range(TWO):
+                    @pl.when(l == k)
+                    def _():
+                        for i in range(homes):
+                            zb[g * homes + i, k * cap:(k + ONE) * cap, pl.ds(at, 256)] = z[i * cap:(i + ONE) * cap].astype(bf16)
                 return 0
 
             lax.fori_loop(0, dm // 256, down, 0)
+            return 0
+
+        lax.fori_loop(0, TWO, expert, 0)
 
         @pl.when(g == 0)
         def _():

time: 503 us -> 496 us (0.986)
  the two profiles are of different devices: /device:TPU:98 before, /device:TPU:97 now
where the time goes in v4:
time: 496 us; the launch traced here: 486 us
  Pallas kernels  449 us (91%)
  other arithmetic  12.1 us (2%)
  waiting for transfers between devices  7.72 us (2%)
  matrix products  6.56 us (1%)
  local copies, waits for them, and re-layouts  5.95 us (1%)
    pallas_call x1, Pallas kernels, moe(): pl.pallas_call(functools.partial(moe_kernel, nx, ny, cap, groups), in_spe...  306 us
    pallas_call x1, Pallas kernels, attention(): pl.pallas_call(attn_kernel, in_specs=[vm] * 9, out_specs=[vm, any_, any_]...  144 us
  transfers between devices with their start and end apart: 1, of which 1 were waited for; matrix products, arithmetic and copies ran while one was open for 1% of the time, Pallas kernels for 0%

profile of v4, /device:TPU:97, one launch (start us, length us, event | category | flops | bytes accessed | tf_op | source)
XLA Modules:
  0.0 486.3 jit_solution(12341104110752038836)
XLA Ops:
  0.0 3.7 fusion.11
  3.8 2.0 pad_maximum_fusion
  5.8 0.0 copy-start.2
  5.8 143.7 %shard_map.145 = (bf16[2048,256]{1,0:T(8,128)(2,1)}, bf16[8,256,2048]{2,1,0:T(8,128)(2,1)}, bf16[8,352,2048]{2,1,0:T(8,128)(2,1)}) custom-call(bf16[256,2048]{1,0:T(8,128)(2,1)} %x_ref.1, f32[1,2048]{1,0:T(1,128)} %bitcast.18, bf16[2048,256]{1,0:T(8,128)(2,1)} %wq_ref.1, bf16[2048,256]{1,0:T(8,128)(2,1)} %wk_ref.1, bf16[2048,256]{1,0:T(8,128)(2,1)} %wv_ref.1, ...), custom_call_target="tpu_custom_call" | custom-call | flops 15032385536 | bytes 67108864 | tf_op jit(solution)/shard_map/pallas_call | solution.py:315
  149.4 0.0 copy-start.1
  149.5 4.6 all-to-all-start
  154.1 0.0 copy-done.2
  154.1 0.2 convolution_add_fusion
  154.3 0.1 select_reduce_fusion
  154.4 0.8 copy.31.code_ref
  155.2 0.0 copy-done.4
  155.2 0.8 copy.32.gate_ref
  156.0 0.0 copy-done.1
  156.0 0.8 copy.29
  156.8 1.9 copy.30
  158.7 0.6 pad.11.idx_ref
  159.3 1.9 fusion.2.ws1_ref
  161.2 7.7 %all-to-all-done = bf16[8,256,256]{2,1,0:T(8,128)(2,1)} async-done(((bf16[8,256,256]{2,1,0:T(8,128)(2,1)}), bf16[8,256,256]{2,1,0:T(8,128)(2,1)}, u32[]{:S(2)}, u32[]{:S(2)}) %all-to-all-start) | async-done | bytes 1048608 | tf_op jit(solution)/shard_map/all_to_all | solution.py:852
  168.9 6.4 %fusion.5 = (f32[256]{0:T(256)S(1)}, bf16[256,2048]{1,0:T(8,128)(2,1)S(1)}) fusion(bf16[8,256,2048]{2,1,0:T(8,128)(2,1)} %get-tuple-element.10, bf16[8,256,256]{2,1,0:T(8,128)(2,1)} %all-to-all-done, bf16[256,2048]{1,0:T(8,128)(2,1)} %x_ref.1), kind=kOutput, calls=%fused_computation.11 | convolution fusion | flops 2150629120 | bytes 11535360 | tf_op jit(solution)/shard_map/dot_general | solution.py:853
  175.3 1.0 copy-done
  176.3 0.0 copy-done.3
  176.3 1.3 fusion.7.t_ref
  177.6 305.5 %shard_map.146 = (f32[256,2048]{1,0:T(8,128)}, bf16[32,256,2048]{2,1,0:T(8,128)(2,1)}, bf16[32,112,2048]{2,1,0:T(8,128)(2,1)}, bf16[8,256,384]{2,1,0:T(8,128)(2,1)}, bf16[9,2,2,112,1024]{4,3,2,1,0:T(8,128)(2,1)}) custom-call(bf16[256,2048]{1,0:T(8,128)(2,1)} %fusion.7.t_ref, s32[8,256]{1,0:T(8,128)} %pad.11.idx_ref, s32[256,6]{1,0:T(8,128)} %copy.31.code_ref, ...), custom_call_target="tpu_custom_call" | custom-call | flops 62008590336 | bytes 57671680 | tf_op jit(solution)/shard_map/pallas_call | solution.py:796
  483.2 3.1 fusion.8
  (8 shorter events, 0.1 us)
Async XLA Ops:
  5.8 148.3 %copy-start.2 = (s32[256,6]{0,1:T(8,128)S(1)}, s32[256,6]{0,1:T(8,128)}, u32[]{:S(2)}) copy-start(s32[256,6]{0,1:T(8,128)} %param.22) | copy-start | bytes 18436
  5.8 149.4 %copy-start.4 = (f32[256,6]{0,1:T(8,128)S(1)}, f32[256,6]{0,1:T(8,128)}, u32[]{:S(2)}) copy-start(f32[256,6]{0,1:T(8,128)} %param.23) | copy-start | bytes 18436
  149.4 6.5 %copy-start.1 = (bf16[2048,352]{0,1:T(8,128)(2,1)S(1)}, bf16[2048,352]{0,1:T(8,128)(2,1)}, u32[]{:S(2)}) copy-start(bf16[2048,352]{0,1:T(8,128)(2,1)} %param.27) | copy-start | bytes 4325380
  149.5 19.4 %all-to-all-start = ((bf16[8,256,256]{2,1,0:T(8,128)(2,1)}), bf16[8,256,256]{2,1,0:T(8,128)(2,1)}, u32[]{:S(2)}, u32[]{:S(2)}) async-start(bf16[8,256,256]{2,1,0:T(8,128)(2,1)} %bitcast.16), calls=%async_computation | async-start | bytes 2097152 | tf_op jit(solution)/shard_map/all_to_all | solution.py:852
  168.9 7.5 %copy-start.3 = (f32[2048]{0:T(1024)S(1)}, f32[2048]{0:T(1024)}, u32[]{:S(2)}) copy-start(f32[2048]{0:T(1024)} %param.21) | copy-start | bytes 24580
  175.3 1.1 copy-start
